TPU v7x, 16 devices: a whole 2x2x2 slice. The times are simulated.
16 devices in a mesh: cp: 16 (over z, y, x, core).
Axes of the slice: x: 2, y: 2, z: 2, core: 2. Of those that a mesh axis runs over, the one named last changes fastest.
Arguments:
- hidden_in: bfloat16 [2, 6144, 2048], P(None, 'cp')
- grad_out: bfloat16 [2, 6144, 2048], P(None, 'cp')
- w_query: bfloat16 [2048, 4096], replicated
- w_key: bfloat16 [2048, 512], replicated
- w_value: bfloat16 [2048, 512], replicated
- w_out: bfloat16 [4096, 2048], replicated
- attn_norm: bfloat16 [2048], replicated
- query_norm: bfloat16 [128], replicated
- key_norm: bfloat16 [128], replicated
Outputs:
- output 1: bfloat16 [2, 6144, 2048], P(None, 'cp')
- output 2: bfloat16 [2, 6144, 2048], P(None, 'cp')
- output 3: float32 [2048, 4096], replicated
- output 4: float32 [2048, 512], replicated
- output 5: float32 [2048, 512], replicated
- output 6: float32 [4096, 2048], replicated
- output 7: float32 [2048], replicated
- output 8: float32 [128], replicated
- output 9: float32 [128], replicated
All inputs are finite; a program needn't handle non-finite values.
Results may differ from a plain program's by a relative error of at most 0.017287.
Values are sent between devices in bfloat16 or wider.
A program may use at most 1 GiB of HBM per device.

v0:
```python
import jax
import jax.numpy as jnp
from jax import lax
from jax.sharding import PartitionSpec as P

HEAD_DIM = 128
ROPE_THETA = 1000000.0
NORM_EPS = 1e-6


def rms_scale(act_vals, norm_gain):
    mean_sq = jnp.mean(act_vals * act_vals, axis=-1, keepdims=True)
    return act_vals * lax.rsqrt(mean_sq + NORM_EPS) * norm_gain


def rope_tables(offset, length):
    inv_freq = ROPE_THETA ** (-jnp.arange(0, HEAD_DIM, 2, dtype=jnp.float32) / HEAD_DIM)
    positions = (offset + jnp.arange(length)).astype(jnp.float32)
    angles = positions[:, None] * inv_freq[None, :]
    angles = jnp.concatenate([angles, angles], axis=-1)
    return jnp.cos(angles), jnp.sin(angles)


def head_finish(pre_proj, norm_gain, cos_t, sin_t):
    normed = rms_scale(pre_proj, norm_gain)
    half_dim = HEAD_DIM // 2
    rotated = jnp.concatenate([-normed[..., half_dim:], normed[..., :half_dim]], axis=-1)
    return normed * cos_t[:, None, :] + rotated * sin_t[:, None, :]


def block_scores(q_blk, k_blk, score_scale):
    return jnp.einsum('bqkgd,bskd->bkgqs', q_blk, k_blk, preferred_element_type=jnp.float32) * score_scale


def softmax_merge(soft_state, q_blk, k_blk, v_blk, score_scale, key_mask):
    run_max, run_sum, weighted = soft_state
    scores = block_scores(q_blk, k_blk, score_scale)
    if key_mask is not None:
        scores = jnp.where(key_mask, scores, -jnp.inf)
    new_max = jnp.maximum(run_max, jnp.max(scores, axis=-1))
    rescale = jnp.exp(run_max - new_max)
    prob_rows = jnp.exp(scores - new_max[..., None])
    run_sum = run_sum * rescale + jnp.sum(prob_rows, axis=-1)
    weighted = weighted * rescale[..., None] + jnp.einsum('bkgqs,bskd->bkgqd', prob_rows.astype(jnp.bfloat16), v_blk, preferred_element_type=jnp.float32)
    return new_max, run_sum, weighted


def block_grads(q_blk, k_blk, v_blk, d_attn, log_sum, row_delta, score_scale, key_mask):
    scores = block_scores(q_blk, k_blk, score_scale)
    if key_mask is not None:
        scores = jnp.where(key_mask, scores, -jnp.inf)
    prob_rows = jnp.exp(scores - log_sum[..., None])
    d_value = jnp.einsum('bkgqs,bkgqd->bskd', prob_rows.astype(jnp.bfloat16), d_attn, preferred_element_type=jnp.float32)
    d_prob = jnp.einsum('bkgqd,bskd->bkgqs', d_attn, v_blk, preferred_element_type=jnp.float32)
    d_score = (prob_rows * (d_prob - row_delta[..., None]) * score_scale).astype(jnp.bfloat16)
    d_query = jnp.einsum('bkgqs,bskd->bqkgd', d_score, k_blk, preferred_element_type=jnp.float32)
    d_key = jnp.einsum('bkgqs,bqkgd->bskd', d_score, q_blk, preferred_element_type=jnp.float32)
    return d_query, d_key, d_value


def solution(mesh):
    axis_size = mesh.shape['cp']
    next_perm = [(dev_id, (dev_id + 1) % axis_size) for dev_id in range(axis_size)]
    seq_spec = P(None, 'cp', None)
    rep_spec = P()

    def local_block(hidden_in, grad_out, w_query, w_key, w_value, w_out, attn_norm, query_norm, key_norm):
        batch_rows, seq_dev, model_dim = hidden_in.shape
        num_heads = w_query.shape[1] // HEAD_DIM
        kv_heads = w_key.shape[1] // HEAD_DIM
        group_size = num_heads // kv_heads
        score_scale = HEAD_DIM ** -0.5
        my_index = lax.axis_index('cp')
        cos_t, sin_t = rope_tables(my_index * seq_dev, seq_dev)
        row_ids = jnp.arange(seq_dev)
        diag_mask = row_ids[:, None] >= row_ids[None, :]

        hidden = hidden_in.astype(jnp.float32)
        normed, norm_pull = jax.vjp(rms_scale, hidden, attn_norm.astype(jnp.float32))
        normed_b = normed.astype(jnp.bfloat16)
        q_pre = jnp.dot(normed_b, w_query, preferred_element_type=jnp.float32).reshape(batch_rows, seq_dev, num_heads, HEAD_DIM)
        k_pre = jnp.dot(normed_b, w_key, preferred_element_type=jnp.float32).reshape(batch_rows, seq_dev, kv_heads, HEAD_DIM)
        v_pre = jnp.dot(normed_b, w_value, preferred_element_type=jnp.float32)
        q_rot, q_pull = jax.vjp(lambda pre_proj, gain_vec: head_finish(pre_proj, gain_vec, cos_t, sin_t), q_pre, query_norm.astype(jnp.float32))
        k_rot, k_pull = jax.vjp(lambda pre_proj, gain_vec: head_finish(pre_proj, gain_vec, cos_t, sin_t), k_pre, key_norm.astype(jnp.float32))
        q_b = q_rot.astype(jnp.bfloat16).reshape(batch_rows, seq_dev, kv_heads, group_size, HEAD_DIM)
        k_b = k_rot.astype(jnp.bfloat16)
        v_b = v_pre.astype(jnp.bfloat16).reshape(batch_rows, seq_dev, kv_heads, HEAD_DIM)

        stat_shape = (batch_rows, kv_heads, group_size, seq_dev)
        start_state = (jnp.full(stat_shape, -jnp.inf, jnp.float32), jnp.zeros(stat_shape, jnp.float32), jnp.zeros(stat_shape + (HEAD_DIM,), jnp.float32))
        soft_state = softmax_merge(start_state, q_b, k_b, v_b, score_scale, diag_mask)

        def fwd_step(step_num, loop_carry):
            soft_in, k_cur, v_cur = loop_carry
            k_cur = lax.ppermute(k_cur, 'cp', next_perm)
            v_cur = lax.ppermute(v_cur, 'cp', next_perm)
            soft_out = lax.cond(step_num <= my_index, lambda state_in: softmax_merge(state_in, q_b, k_cur, v_cur, score_scale, None), lambda state_in: state_in, soft_in)
            return soft_out, k_cur, v_cur

        fwd_out = lax.fori_loop(1, axis_size, fwd_step, (soft_state, k_b, v_b))
        run_max, run_sum, weighted = fwd_out[0]
        attn_out = (weighted / run_sum[..., None]).astype(jnp.bfloat16)
        log_sum = run_max + jnp.log(run_sum)
        w_out4 = w_out.reshape(kv_heads, group_size, HEAD_DIM, model_dim)
        projected = jnp.einsum('bkgqd,kgdm->bqm', attn_out, w_out4, preferred_element_type=jnp.float32)
        hidden_out = (hidden + projected).astype(jnp.bfloat16)

        d_attn = jnp.einsum('bqm,kgdm->bkgqd', grad_out, w_out4, preferred_element_type=jnp.float32).astype(jnp.bfloat16)
        wgrad_out = jnp.einsum('bkgqd,bqm->kgdm', attn_out, grad_out, preferred_element_type=jnp.float32).reshape(num_heads * HEAD_DIM, model_dim)
        row_delta = jnp.sum(d_attn.astype(jnp.float32) * attn_out.astype(jnp.float32), axis=-1)
        d_query, d_key, d_value = block_grads(q_b, k_b, v_b, d_attn, log_sum, row_delta, score_scale, diag_mask)

        def bwd_step(step_num, loop_carry):
            dq_acc, k_cur, v_cur, dk_cur, dv_cur = loop_carry
            k_cur = lax.ppermute(k_cur, 'cp', next_perm)
            v_cur = lax.ppermute(v_cur, 'cp', next_perm)
            dk_cur = lax.ppermute(dk_cur, 'cp', next_perm)
            dv_cur = lax.ppermute(dv_cur, 'cp', next_perm)

            def add_block(grad_parts):
                dq_new, dk_new, dv_new = block_grads(q_b, k_cur, v_cur, d_attn, log_sum, row_delta, score_scale, None)
                return grad_parts[0] + dq_new, grad_parts[1] + dk_new, grad_parts[2] + dv_new

            dq_acc, dk_cur, dv_cur = lax.cond(step_num <= my_index, add_block, lambda grad_parts: grad_parts, (dq_acc, dk_cur, dv_cur))
            return dq_acc, k_cur, v_cur, dk_cur, dv_cur

        bwd_out = lax.fori_loop(1, axis_size, bwd_step, (d_query, k_b, v_b, d_key, d_value))
        d_query = bwd_out[0]
        d_key = lax.ppermute(bwd_out[3], 'cp', next_perm)
        d_value = lax.ppermute(bwd_out[4], 'cp', next_perm)

        dq_round = d_query.astype(jnp.bfloat16).astype(jnp.float32).reshape(batch_rows, seq_dev, num_heads, HEAD_DIM)
        dq_pre, ngrad_query = q_pull(dq_round)
        dk_pre, ngrad_key = k_pull(d_key.astype(jnp.bfloat16).astype(jnp.float32))
        dq_flat = dq_pre.astype(jnp.bfloat16).reshape(batch_rows, seq_dev, num_heads * HEAD_DIM)
        dk_flat = dk_pre.astype(jnp.bfloat16).reshape(batch_rows, seq_dev, kv_heads * HEAD_DIM)
        dv_flat = d_value.astype(jnp.bfloat16).reshape(batch_rows, seq_dev, kv_heads * HEAD_DIM)
        wgrad_query = jnp.einsum('bsd,bsf->df', normed_b, dq_flat, preferred_element_type=jnp.float32)
        wgrad_key = jnp.einsum('bsd,bsf->df', normed_b, dk_flat, preferred_element_type=jnp.float32)
        wgrad_value = jnp.einsum('bsd,bsf->df', normed_b, dv_flat, preferred_element_type=jnp.float32)
        d_normed = (jnp.einsum('bsf,df->bsd', dq_flat, w_query, preferred_element_type=jnp.float32) + jnp.einsum('bsf,df->bsd', dk_flat, w_key, preferred_element_type=jnp.float32) + jnp.einsum('bsf,df->bsd', dv_flat, w_value, preferred_element_type=jnp.float32)).astype(jnp.bfloat16).astype(jnp.float32)
        d_hidden, ngrad_attn = norm_pull(d_normed)
        grad_in = (grad_out.astype(jnp.float32) + d_hidden).astype(jnp.bfloat16)
        summed = lax.psum((wgrad_query, wgrad_key, wgrad_value, wgrad_out, ngrad_attn, ngrad_query, ngrad_key), 'cp')
        return (hidden_out, grad_in) + tuple(summed)

    return jax.shard_map(local_block, mesh=mesh, in_specs=(seq_spec, seq_spec) + (rep_spec,) * 7, out_specs=(seq_spec, seq_spec) + (rep_spec,) * 7, check_vma=False)
```

profile of v0, /device:TPU:0, one launch (start us, length us, event | category | flops | bytes accessed | tf_op | source)
XLA Modules:
  0.0 4670.4 jit_solution(1257027156339170212)
XLA Ops:
  43.0 20.4 fusion.43
  137.4 17.9 fusion.47
  155.3 17.5 fusion.29
  172.8 16.7 fusion.27
  189.6 20.5 broadcast_add_fusion
  210.1 1147.6 %while.42 = (s32[]{:T(128)}, f32[2,4,8,384]{3,2,1,0:T(8,128)S(1)}, f32[2,4,8,384]{3,2,1,0:T(8,128)S(1)}, f32[2,4,8,384,128]{4,3,2,1,0:T(8,128)}, bf16[2,384,4,12...) while((s32[]{:T(128)}, f32[2,4,8,384]{3,2,1,0:T(8,128)S(1)}, ...), condition=%wide.region_10.11_spmd, body=%wide.region_5.10_spmd.sunk | while | flops 4913676288 | bytes 157286704 | solution.py:101
  236.0 56.4 %collective-permute-start.1 = (bf16[2,384,4,128]{3,1,2,0:T(8,128)(2,1)}, bf16[2,384,4,128]{3,1,2,0:T(8,128)(2,1)}, u32[]{:S(2)}, u32[]{:S(2)}) collective-permute-start(bf16[2,384,4,128]{3,1,2,0:T(8,128)(2,1)} %get-tuple-element.743), channel_id=1, source_target_pairs={{0,1},{1,2},{2,3},{3,4},{4,5},{5,6},{6,7},{7,8},{8,9},{9,10},{10,1... | collective-permute-start | bytes 2359304 | tf_op jit(solution)/shard_map/while/body/eval_jaxpr/ppermute | solution.py:97
  315.2 61.0 %collective-permute-start = (bf16[2,384,4,128]{3,1,2,0:T(8,128)(2,1)}, bf16[2,384,4,128]{3,1,2,0:T(8,128)(2,1)S(1)}, u32[]{:S(2)}, u32[]{:S(2)}) collective-permute-start(bf16[2,384,4,128]{3,1,2,0:T(8,128)(2,1)} %get-tuple-element.742), channel_id=1, source_target_pairs={{0,1},{1,2},{2,3},{3,4},{4,5},{5,6},{6,7},{7,8},{8,9},{9,10},{10,1... | collective-permute-start | bytes 2359304 | tf_op jit(solution)/shard_map/while/body/eval_jaxpr/ppermute | solution.py:96
  399.0 62.0 %collective-permute-done.1 = bf16[2,384,4,128]{3,1,2,0:T(8,128)(2,1)} collective-permute-done((bf16[2,384,4,128]{3,1,2,0:T(8,128)(2,1)}, bf16[2,384,4,128]{3,1,2,0:T(8,128)(2,1)}, u32[]{:S(2)}, u32[]{:S(2)}) %collective-permute-start.1) | collective-permute-done | bytes 786464 | tf_op jit(solution)/shard_map/while/body/eval_jaxpr/ppermute | solution.py:97
  472.8 67.0 %collective-permute-done.1 = bf16[2,384,4,128]{3,1,2,0:T(8,128)(2,1)} collective-permute-done((bf16[2,384,4,128]{3,1,2,0:T(8,128)(2,1)}, bf16[2,384,4,128]{3,1,2,0:T(8,128)(2,1)}, u32[]{:S(2)}, u32[]{:S(2)}) %collective-permute-start.1) | collective-permute-done | bytes 786464 | tf_op jit(solution)/shard_map/while/body/eval_jaxpr/ppermute | solution.py:97
  551.1 67.4 %collective-permute-done.1 = bf16[2,384,4,128]{3,1,2,0:T(8,128)(2,1)} collective-permute-done((bf16[2,384,4,128]{3,1,2,0:T(8,128)(2,1)}, bf16[2,384,4,128]{3,1,2,0:T(8,128)(2,1)}, u32[]{:S(2)}, u32[]{:S(2)}) %collective-permute-start.1) | collective-permute-done | bytes 786464 | tf_op jit(solution)/shard_map/while/body/eval_jaxpr/ppermute | solution.py:97
  629.9 67.4 %collective-permute-done.1 = bf16[2,384,4,128]{3,1,2,0:T(8,128)(2,1)} collective-permute-done((bf16[2,384,4,128]{3,1,2,0:T(8,128)(2,1)}, bf16[2,384,4,128]{3,1,2,0:T(8,128)(2,1)}, u32[]{:S(2)}, u32[]{:S(2)}) %collective-permute-start.1) | collective-permute-done | bytes 786464 | tf_op jit(solution)/shard_map/while/body/eval_jaxpr/ppermute | solution.py:97
  708.7 68.6 %collective-permute-done.1 = bf16[2,384,4,128]{3,1,2,0:T(8,128)(2,1)} collective-permute-done((bf16[2,384,4,128]{3,1,2,0:T(8,128)(2,1)}, bf16[2,384,4,128]{3,1,2,0:T(8,128)(2,1)}, u32[]{:S(2)}, u32[]{:S(2)}) %collective-permute-start.1) | collective-permute-done | bytes 786464 | tf_op jit(solution)/shard_map/while/body/eval_jaxpr/ppermute | solution.py:97
  788.7 69.9 %collective-permute-done.1 = bf16[2,384,4,128]{3,1,2,0:T(8,128)(2,1)} collective-permute-done((bf16[2,384,4,128]{3,1,2,0:T(8,128)(2,1)}, bf16[2,384,4,128]{3,1,2,0:T(8,128)(2,1)}, u32[]{:S(2)}, u32[]{:S(2)}) %collective-permute-start.1) | collective-permute-done | bytes 786464 | tf_op jit(solution)/shard_map/while/body/eval_jaxpr/ppermute | solution.py:97
  870.0 69.9 %collective-permute-done.1 = bf16[2,384,4,128]{3,1,2,0:T(8,128)(2,1)} collective-permute-done((bf16[2,384,4,128]{3,1,2,0:T(8,128)(2,1)}, bf16[2,384,4,128]{3,1,2,0:T(8,128)(2,1)}, u32[]{:S(2)}, u32[]{:S(2)}) %collective-permute-start.1) | collective-permute-done | bytes 786464 | tf_op jit(solution)/shard_map/while/body/eval_jaxpr/ppermute | solution.py:97
  951.3 69.9 %collective-permute-done.1 = bf16[2,384,4,128]{3,1,2,0:T(8,128)(2,1)} collective-permute-done((bf16[2,384,4,128]{3,1,2,0:T(8,128)(2,1)}, bf16[2,384,4,128]{3,1,2,0:T(8,128)(2,1)}, u32[]{:S(2)}, u32[]{:S(2)}) %collective-permute-start.1) | collective-permute-done | bytes 786464 | tf_op jit(solution)/shard_map/while/body/eval_jaxpr/ppermute | solution.py:97
  1032.6 69.9 %collective-permute-done.1 = bf16[2,384,4,128]{3,1,2,0:T(8,128)(2,1)} collective-permute-done((bf16[2,384,4,128]{3,1,2,0:T(8,128)(2,1)}, bf16[2,384,4,128]{3,1,2,0:T(8,128)(2,1)}, u32[]{:S(2)}, u32[]{:S(2)}) %collective-permute-start.1) | collective-permute-done | bytes 786464 | tf_op jit(solution)/shard_map/while/body/eval_jaxpr/ppermute | solution.py:97
  1113.9 69.9 %collective-permute-done.1 = bf16[2,384,4,128]{3,1,2,0:T(8,128)(2,1)} collective-permute-done((bf16[2,384,4,128]{3,1,2,0:T(8,128)(2,1)}, bf16[2,384,4,128]{3,1,2,0:T(8,128)(2,1)}, u32[]{:S(2)}, u32[]{:S(2)}) %collective-permute-start.1) | collective-permute-done | bytes 786464 | tf_op jit(solution)/shard_map/while/body/eval_jaxpr/ppermute | solution.py:97
  1195.2 69.9 %collective-permute-done.1 = bf16[2,384,4,128]{3,1,2,0:T(8,128)(2,1)} collective-permute-done((bf16[2,384,4,128]{3,1,2,0:T(8,128)(2,1)}, bf16[2,384,4,128]{3,1,2,0:T(8,128)(2,1)}, u32[]{:S(2)}, u32[]{:S(2)}) %collective-permute-start.1) | collective-permute-done | bytes 786464 | tf_op jit(solution)/shard_map/while/body/eval_jaxpr/ppermute | solution.py:97
  1276.4 69.9 %collective-permute-done.1 = bf16[2,384,4,128]{3,1,2,0:T(8,128)(2,1)} collective-permute-done((bf16[2,384,4,128]{3,1,2,0:T(8,128)(2,1)}, bf16[2,384,4,128]{3,1,2,0:T(8,128)(2,1)}, u32[]{:S(2)}, u32[]{:S(2)}) %collective-permute-start.1) | collective-permute-done | bytes 786464 | tf_op jit(solution)/shard_map/while/body/eval_jaxpr/ppermute | solution.py:97
  1370.5 23.9 multiply_reduce_fusion.2
  1403.1 18.2 fusion.81
  1421.3 26.9 multiply_convert_fusion.1
  1460.6 14.7 convolution_bitcast_fusion.1
  1493.9 2235.4 %while.43 = (s32[]{:T(128)}, f32[2,384,4,8,128]{4,1,3,2,0:T(8,128)}, bf16[2,384,4,128]{3,1,2,0:T(8,128)(2,1)}, bf16[2,384,4,128]{3,1,2,0:T(8,128)(2,1)}, f32[2,3...) while((s32[]{:T(128)}, ...), condition=%wide.region_15.16_spmd, body=%wide.region_12.15_spmd.sunk | while | flops 12168462336 | bytes 258638320 | solution.py:128
  1494.7 103.0 %collective-permute-done.5 = bf16[2,384,4,128]{3,1,2,0:T(8,128)(2,1)} collective-permute-done((bf16[2,384,4,128]{3,1,2,0:T(8,128)(2,1)}, bf16[2,384,4,128]{3,1,2,0:T(8,128)(2,1)}, u32[]{:S(2)}, u32[]{:S(2)}) %collective-permute-start.5) | collective-permute-done | bytes 786464 | tf_op jit(solution)/shard_map/while/body/eval_jaxpr/ppermute | solution.py:117
  1613.1 135.8 %collective-permute-done.5 = bf16[2,384,4,128]{3,1,2,0:T(8,128)(2,1)} collective-permute-done((bf16[2,384,4,128]{3,1,2,0:T(8,128)(2,1)}, bf16[2,384,4,128]{3,1,2,0:T(8,128)(2,1)}, u32[]{:S(2)}, u32[]{:S(2)}) %collective-permute-start.5) | collective-permute-done | bytes 786464 | tf_op jit(solution)/shard_map/while/body/eval_jaxpr/ppermute | solution.py:117
  1764.3 135.8 %collective-permute-done.5 = bf16[2,384,4,128]{3,1,2,0:T(8,128)(2,1)} collective-permute-done((bf16[2,384,4,128]{3,1,2,0:T(8,128)(2,1)}, bf16[2,384,4,128]{3,1,2,0:T(8,128)(2,1)}, u32[]{:S(2)}, u32[]{:S(2)}) %collective-permute-start.5) | collective-permute-done | bytes 786464 | tf_op jit(solution)/shard_map/while/body/eval_jaxpr/ppermute | solution.py:117
  1915.4 135.8 %collective-permute-done.5 = bf16[2,384,4,128]{3,1,2,0:T(8,128)(2,1)} collective-permute-done((bf16[2,384,4,128]{3,1,2,0:T(8,128)(2,1)}, bf16[2,384,4,128]{3,1,2,0:T(8,128)(2,1)}, u32[]{:S(2)}, u32[]{:S(2)}) %collective-permute-start.5) | collective-permute-done | bytes 786464 | tf_op jit(solution)/shard_map/while/body/eval_jaxpr/ppermute | solution.py:117
  2066.6 135.8 %collective-permute-done.5 = bf16[2,384,4,128]{3,1,2,0:T(8,128)(2,1)} collective-permute-done((bf16[2,384,4,128]{3,1,2,0:T(8,128)(2,1)}, bf16[2,384,4,128]{3,1,2,0:T(8,128)(2,1)}, u32[]{:S(2)}, u32[]{:S(2)}) %collective-permute-start.5) | collective-permute-done | bytes 786464 | tf_op jit(solution)/shard_map/while/body/eval_jaxpr/ppermute | solution.py:117
  2217.8 135.8 %collective-permute-done.5 = bf16[2,384,4,128]{3,1,2,0:T(8,128)(2,1)} collective-permute-done((bf16[2,384,4,128]{3,1,2,0:T(8,128)(2,1)}, bf16[2,384,4,128]{3,1,2,0:T(8,128)(2,1)}, u32[]{:S(2)}, u32[]{:S(2)}) %collective-permute-start.5) | collective-permute-done | bytes 786464 | tf_op jit(solution)/shard_map/while/body/eval_jaxpr/ppermute | solution.py:117
  2369.0 135.8 %collective-permute-done.5 = bf16[2,384,4,128]{3,1,2,0:T(8,128)(2,1)} collective-permute-done((bf16[2,384,4,128]{3,1,2,0:T(8,128)(2,1)}, bf16[2,384,4,128]{3,1,2,0:T(8,128)(2,1)}, u32[]{:S(2)}, u32[]{:S(2)}) %collective-permute-start.5) | collective-permute-done | bytes 786464 | tf_op jit(solution)/shard_map/while/body/eval_jaxpr/ppermute | solution.py:117
  2520.1 135.8 %collective-permute-done.5 = bf16[2,384,4,128]{3,1,2,0:T(8,128)(2,1)} collective-permute-done((bf16[2,384,4,128]{3,1,2,0:T(8,128)(2,1)}, bf16[2,384,4,128]{3,1,2,0:T(8,128)(2,1)}, u32[]{:S(2)}, u32[]{:S(2)}) %collective-permute-start.5) | collective-permute-done | bytes 786464 | tf_op jit(solution)/shard_map/while/body/eval_jaxpr/ppermute | solution.py:117
  2671.3 135.8 %collective-permute-done.5 = bf16[2,384,4,128]{3,1,2,0:T(8,128)(2,1)} collective-permute-done((bf16[2,384,4,128]{3,1,2,0:T(8,128)(2,1)}, bf16[2,384,4,128]{3,1,2,0:T(8,128)(2,1)}, u32[]{:S(2)}, u32[]{:S(2)}) %collective-permute-start.5) | collective-permute-done | bytes 786464 | tf_op jit(solution)/shard_map/while/body/eval_jaxpr/ppermute | solution.py:117
  2822.5 135.8 %collective-permute-done.5 = bf16[2,384,4,128]{3,1,2,0:T(8,128)(2,1)} collective-permute-done((bf16[2,384,4,128]{3,1,2,0:T(8,128)(2,1)}, bf16[2,384,4,128]{3,1,2,0:T(8,128)(2,1)}, u32[]{:S(2)}, u32[]{:S(2)}) %collective-permute-start.5) | collective-permute-done | bytes 786464 | tf_op jit(solution)/shard_map/while/body/eval_jaxpr/ppermute | solution.py:117
  2973.7 135.8 %collective-permute-done.5 = bf16[2,384,4,128]{3,1,2,0:T(8,128)(2,1)} collective-permute-done((bf16[2,384,4,128]{3,1,2,0:T(8,128)(2,1)}, bf16[2,384,4,128]{3,1,2,0:T(8,128)(2,1)}, u32[]{:S(2)}, u32[]{:S(2)}) %collective-permute-start.5) | collective-permute-done | bytes 786464 | tf_op jit(solution)/shard_map/while/body/eval_jaxpr/ppermute | solution.py:117
  3124.8 135.8 %collective-permute-done.5 = bf16[2,384,4,128]{3,1,2,0:T(8,128)(2,1)} collective-permute-done((bf16[2,384,4,128]{3,1,2,0:T(8,128)(2,1)}, bf16[2,384,4,128]{3,1,2,0:T(8,128)(2,1)}, u32[]{:S(2)}, u32[]{:S(2)}) %collective-permute-start.5) | collective-permute-done | bytes 786464 | tf_op jit(solution)/shard_map/while/body/eval_jaxpr/ppermute | solution.py:117
  3276.0 135.8 %collective-permute-done.5 = bf16[2,384,4,128]{3,1,2,0:T(8,128)(2,1)} collective-permute-done((bf16[2,384,4,128]{3,1,2,0:T(8,128)(2,1)}, bf16[2,384,4,128]{3,1,2,0:T(8,128)(2,1)}, u32[]{:S(2)}, u32[]{:S(2)}) %collective-permute-start.5) | collective-permute-done | bytes 786464 | tf_op jit(solution)/shard_map/while/body/eval_jaxpr/ppermute | solution.py:117
  3427.2 135.8 %collective-permute-done.5 = bf16[2,384,4,128]{3,1,2,0:T(8,128)(2,1)} collective-permute-done((bf16[2,384,4,128]{3,1,2,0:T(8,128)(2,1)}, bf16[2,384,4,128]{3,1,2,0:T(8,128)(2,1)}, u32[]{:S(2)}, u32[]{:S(2)}) %collective-permute-start.5) | collective-permute-done | bytes 786464 | tf_op jit(solution)/shard_map/while/body/eval_jaxpr/ppermute | solution.py:117
  3578.4 135.8 %collective-permute-done.5 = bf16[2,384,4,128]{3,1,2,0:T(8,128)(2,1)} collective-permute-done((bf16[2,384,4,128]{3,1,2,0:T(8,128)(2,1)}, bf16[2,384,4,128]{3,1,2,0:T(8,128)(2,1)}, u32[]{:S(2)}, u32[]{:S(2)}) %collective-permute-start.5) | collective-permute-done | bytes 786464 | tf_op jit(solution)/shard_map/while/body/eval_jaxpr/ppermute | solution.py:117
  3780.3 22.8 multiply_reduce_fusion
  3803.2 18.8 fusion.66
  3831.9 23.4 convolution_bitcast_fusion
  3867.4 20.4 fusion.41
  3887.8 20.1 fusion.57
  3917.3 123.9 %all-reduce.4 = (f32[2048]{0:T(1024)}, f32[128]{0:T(128)}, f32[128]{0:T(128)}) all-reduce(f32[2048]{0:T(1024)S(1)} %get-tuple-element.514, f32[128]{0:T(128)S(1)} %get-tuple-element.512, f32[128]{0:T(128)S(1)} %get-tuple-element.516), channel_id=1, replica_groups=mesh['cp'=16] {'cp'}, use_global_device_ids=true, to_apply=%region_24.25 | all-reduce | flops 2304 | bytes 18432 | tf_op jit(solution)/shard_map/psum | solution.py:145
  4047.2 566.9 %all-reduce.8.cloned.1.call-done = (f32[2048,4096]{1,0:T(8,128)}, f32[2048,512]{1,0:T(8,128)}, f32[2048,512]{1,0:T(8,128)}, f32[4096,2048]{1,0:T(8,128)}) async-done(((f32[2048,4096]{1,0:T(8,128)}, f32[2048,512]{1,0:T(8,128)}, f32[2048,512]{1,0:T(8,128)}, f32[4096,2048]{1,0:T(8,128)}), (f32[2048,4096]{1,0:T(8,128)}, f32[2048,512]{1,0:T(8,128)}, f32[2048,512]{1,0:T(8,128)}, ...) | async-done | bytes 75497488 | tf_op jit(solution)/shard_map/psum | solution.py:145
  4614.1 26.7 copy.383
  (505 shorter events, 711.0 us)
Async XLA Ops:
  7.2 4606.9 %all-reduce.8.cloned.1.call-start = ((), (), s32[]{:S(2)}) async-start(), calls=%async_computation | async-start | bytes 150994944 | tf_op jit(solution)/shard_map/psum | solution.py:145
  1612.5 145.8 %collective-permute-start.3 = (f32[2,384,4,128]{3,1,2,0:T(8,128)}, f32[2,384,4,128]{3,1,2,0:T(8,128)}, u32[]{:S(2)}, u32[]{:S(2)}) collective-permute-start(f32[2,384,4,128]{3,1,2,0:T(8,128)} %get-tuple-element.773), channel_id=1, source_target_pairs={{0,1},{1,2},{2,3},{3,4},{4,5},{5,6},{6,7},{7,8},{8,9},{9,10},{10,1... | collective-permute-start | bytes 4718600 | tf_op jit(solution)/shard_map/while/body/eval_jaxpr/ppermute | solution.py:119
  1612.5 145.8 %collective-permute-start.2 = (f32[2,384,4,128]{3,1,2,0:T(8,128)}, f32[2,384,4,128]{3,1,2,0:T(8,128)}, u32[]{:S(2)}, u32[]{:S(2)}) collective-permute-start(f32[2,384,4,128]{3,1,2,0:T(8,128)} %get-tuple-element.772), channel_id=1, source_target_pairs={{0,1},{1,2},{2,3},{3,4},{4,5},{5,6},{6,7},{7,8},{8,9},{9,10},{10,1... | collective-permute-start | bytes 4718600 | tf_op jit(solution)/shard_map/while/body/eval_jaxpr/ppermute | solution.py:118
  1613.1 144.2 %collective-permute-start.4 = (bf16[2,384,4,128]{3,1,2,0:T(8,128)(2,1)}, bf16[2,384,4,128]{3,1,2,0:T(8,128)(2,1)S(1)}, u32[]{:S(2)}, u32[]{:S(2)}) collective-permute-start(bf16[2,384,4,128]{3,1,2,0:T(8,128)(2,1)} %get-tuple-element.770), channel_id=1, source_target_pairs={{0,1},{1,2},{2,3},{3,4},{4,5},{5,6},{6,7},{7,8},{8,9},{9,10},{10,1... | collective-permute-start | bytes 2359304 | tf_op jit(solution)/shard_map/while/body/eval_jaxpr/ppermute | solution.py:116
  1763.6 145.8 %collective-permute-start.3 = (f32[2,384,4,128]{3,1,2,0:T(8,128)}, f32[2,384,4,128]{3,1,2,0:T(8,128)}, u32[]{:S(2)}, u32[]{:S(2)}) collective-permute-start(f32[2,384,4,128]{3,1,2,0:T(8,128)} %get-tuple-element.773), channel_id=1, source_target_pairs={{0,1},{1,2},{2,3},{3,4},{4,5},{5,6},{6,7},{7,8},{8,9},{9,10},{10,1... | collective-permute-start | bytes 4718600 | tf_op jit(solution)/shard_map/while/body/eval_jaxpr/ppermute | solution.py:119
  1763.6 145.8 %collective-permute-start.2 = (f32[2,384,4,128]{3,1,2,0:T(8,128)}, f32[2,384,4,128]{3,1,2,0:T(8,128)}, u32[]{:S(2)}, u32[]{:S(2)}) collective-permute-start(f32[2,384,4,128]{3,1,2,0:T(8,128)} %get-tuple-element.772), channel_id=1, source_target_pairs={{0,1},{1,2},{2,3},{3,4},{4,5},{5,6},{6,7},{7,8},{8,9},{9,10},{10,1... | collective-permute-start | bytes 4718600 | tf_op jit(solution)/shard_map/while/body/eval_jaxpr/ppermute | solution.py:118
  1764.3 144.2 %collective-permute-start.4 = (bf16[2,384,4,128]{3,1,2,0:T(8,128)(2,1)}, bf16[2,384,4,128]{3,1,2,0:T(8,128)(2,1)S(1)}, u32[]{:S(2)}, u32[]{:S(2)}) collective-permute-start(bf16[2,384,4,128]{3,1,2,0:T(8,128)(2,1)} %get-tuple-element.770), channel_id=1, source_target_pairs={{0,1},{1,2},{2,3},{3,4},{4,5},{5,6},{6,7},{7,8},{8,9},{9,10},{10,1... | collective-permute-start | bytes 2359304 | tf_op jit(solution)/shard_map/while/body/eval_jaxpr/ppermute | solution.py:116
  1914.8 145.8 %collective-permute-start.3 = (f32[2,384,4,128]{3,1,2,0:T(8,128)}, f32[2,384,4,128]{3,1,2,0:T(8,128)}, u32[]{:S(2)}, u32[]{:S(2)}) collective-permute-start(f32[2,384,4,128]{3,1,2,0:T(8,128)} %get-tuple-element.773), channel_id=1, source_target_pairs={{0,1},{1,2},{2,3},{3,4},{4,5},{5,6},{6,7},{7,8},{8,9},{9,10},{10,1... | collective-permute-start | bytes 4718600 | tf_op jit(solution)/shard_map/while/body/eval_jaxpr/ppermute | solution.py:119
  1914.8 145.8 %collective-permute-start.2 = (f32[2,384,4,128]{3,1,2,0:T(8,128)}, f32[2,384,4,128]{3,1,2,0:T(8,128)}, u32[]{:S(2)}, u32[]{:S(2)}) collective-permute-start(f32[2,384,4,128]{3,1,2,0:T(8,128)} %get-tuple-element.772), channel_id=1, source_target_pairs={{0,1},{1,2},{2,3},{3,4},{4,5},{5,6},{6,7},{7,8},{8,9},{9,10},{10,1... | collective-permute-start | bytes 4718600 | tf_op jit(solution)/shard_map/while/body/eval_jaxpr/ppermute | solution.py:118
  1914.9 136.4 %collective-permute-start.5 = (bf16[2,384,4,128]{3,1,2,0:T(8,128)(2,1)}, bf16[2,384,4,128]{3,1,2,0:T(8,128)(2,1)}, u32[]{:S(2)}, u32[]{:S(2)}) collective-permute-start(bf16[2,384,4,128]{3,1,2,0:T(8,128)(2,1)} %get-tuple-element.771), channel_id=1, source_target_pairs={{0,1},{1,2},{2,3},{3,4},{4,5},{5,6},{6,7},{7,8},{8,9},{9,10},{10,1... | collective-permute-start | bytes 2359304 | tf_op jit(solution)/shard_map/while/body/eval_jaxpr/ppermute | solution.py:117
  1915.4 144.2 %collective-permute-start.4 = (bf16[2,384,4,128]{3,1,2,0:T(8,128)(2,1)}, bf16[2,384,4,128]{3,1,2,0:T(8,128)(2,1)S(1)}, u32[]{:S(2)}, u32[]{:S(2)}) collective-permute-start(bf16[2,384,4,128]{3,1,2,0:T(8,128)(2,1)} %get-tuple-element.770), channel_id=1, source_target_pairs={{0,1},{1,2},{2,3},{3,4},{4,5},{5,6},{6,7},{7,8},{8,9},{9,10},{10,1... | collective-permute-start | bytes 2359304 | tf_op jit(solution)/shard_map/while/body/eval_jaxpr/ppermute | solution.py:116
  2066.0 145.8 %collective-permute-start.3 = (f32[2,384,4,128]{3,1,2,0:T(8,128)}, f32[2,384,4,128]{3,1,2,0:T(8,128)}, u32[]{:S(2)}, u32[]{:S(2)}) collective-permute-start(f32[2,384,4,128]{3,1,2,0:T(8,128)} %get-tuple-element.773), channel_id=1, source_target_pairs={{0,1},{1,2},{2,3},{3,4},{4,5},{5,6},{6,7},{7,8},{8,9},{9,10},{10,1... | collective-permute-start | bytes 4718600 | tf_op jit(solution)/shard_map/while/body/eval_jaxpr/ppermute | solution.py:119
  2066.0 145.8 %collective-permute-start.2 = (f32[2,384,4,128]{3,1,2,0:T(8,128)}, f32[2,384,4,128]{3,1,2,0:T(8,128)}, u32[]{:S(2)}, u32[]{:S(2)}) collective-permute-start(f32[2,384,4,128]{3,1,2,0:T(8,128)} %get-tuple-element.772), channel_id=1, source_target_pairs={{0,1},{1,2},{2,3},{3,4},{4,5},{5,6},{6,7},{7,8},{8,9},{9,10},{10,1... | collective-permute-start | bytes 4718600 | tf_op jit(solution)/shard_map/while/body/eval_jaxpr/ppermute | solution.py:118
  2066.6 144.2 %collective-permute-start.4 = (bf16[2,384,4,128]{3,1,2,0:T(8,128)(2,1)}, bf16[2,384,4,128]{3,1,2,0:T(8,128)(2,1)S(1)}, u32[]{:S(2)}, u32[]{:S(2)}) collective-permute-start(bf16[2,384,4,128]{3,1,2,0:T(8,128)(2,1)} %get-tuple-element.770), channel_id=1, source_target_pairs={{0,1},{1,2},{2,3},{3,4},{4,5},{5,6},{6,7},{7,8},{8,9},{9,10},{10,1... | collective-permute-start | bytes 2359304 | tf_op jit(solution)/shard_map/while/body/eval_jaxpr/ppermute | solution.py:116
  2217.2 145.8 %collective-permute-start.3 = (f32[2,384,4,128]{3,1,2,0:T(8,128)}, f32[2,384,4,128]{3,1,2,0:T(8,128)}, u32[]{:S(2)}, u32[]{:S(2)}) collective-permute-start(f32[2,384,4,128]{3,1,2,0:T(8,128)} %get-tuple-element.773), channel_id=1, source_target_pairs={{0,1},{1,2},{2,3},{3,4},{4,5},{5,6},{6,7},{7,8},{8,9},{9,10},{10,1... | collective-permute-start | bytes 4718600 | tf_op jit(solution)/shard_map/while/body/eval_jaxpr/ppermute | solution.py:119
  2217.2 145.8 %collective-permute-start.2 = (f32[2,384,4,128]{3,1,2,0:T(8,128)}, f32[2,384,4,128]{3,1,2,0:T(8,128)}, u32[]{:S(2)}, u32[]{:S(2)}) collective-permute-start(f32[2,384,4,128]{3,1,2,0:T(8,128)} %get-tuple-element.772), channel_id=1, source_target_pairs={{0,1},{1,2},{2,3},{3,4},{4,5},{5,6},{6,7},{7,8},{8,9},{9,10},{10,1... | collective-permute-start | bytes 4718600 | tf_op jit(solution)/shard_map/while/body/eval_jaxpr/ppermute | solution.py:118
  2217.2 136.4 %collective-permute-start.5 = (bf16[2,384,4,128]{3,1,2,0:T(8,128)(2,1)}, bf16[2,384,4,128]{3,1,2,0:T(8,128)(2,1)}, u32[]{:S(2)}, u32[]{:S(2)}) collective-permute-start(bf16[2,384,4,128]{3,1,2,0:T(8,128)(2,1)} %get-tuple-element.771), channel_id=1, source_target_pairs={{0,1},{1,2},{2,3},{3,4},{4,5},{5,6},{6,7},{7,8},{8,9},{9,10},{10,1... | collective-permute-start | bytes 2359304 | tf_op jit(solution)/shard_map/while/body/eval_jaxpr/ppermute | solution.py:117
  2217.8 144.2 %collective-permute-start.4 = (bf16[2,384,4,128]{3,1,2,0:T(8,128)(2,1)}, bf16[2,384,4,128]{3,1,2,0:T(8,128)(2,1)S(1)}, u32[]{:S(2)}, u32[]{:S(2)}) collective-permute-start(bf16[2,384,4,128]{3,1,2,0:T(8,128)(2,1)} %get-tuple-element.770), channel_id=1, source_target_pairs={{0,1},{1,2},{2,3},{3,4},{4,5},{5,6},{6,7},{7,8},{8,9},{9,10},{10,1... | collective-permute-start | bytes 2359304 | tf_op jit(solution)/shard_map/while/body/eval_jaxpr/ppermute | solution.py:116
  2368.3 145.8 %collective-permute-start.3 = (f32[2,384,4,128]{3,1,2,0:T(8,128)}, f32[2,384,4,128]{3,1,2,0:T(8,128)}, u32[]{:S(2)}, u32[]{:S(2)}) collective-permute-start(f32[2,384,4,128]{3,1,2,0:T(8,128)} %get-tuple-element.773), channel_id=1, source_target_pairs={{0,1},{1,2},{2,3},{3,4},{4,5},{5,6},{6,7},{7,8},{8,9},{9,10},{10,1... | collective-permute-start | bytes 4718600 | tf_op jit(solution)/shard_map/while/body/eval_jaxpr/ppermute | solution.py:119
  2368.3 145.8 %collective-permute-start.2 = (f32[2,384,4,128]{3,1,2,0:T(8,128)}, f32[2,384,4,128]{3,1,2,0:T(8,128)}, u32[]{:S(2)}, u32[]{:S(2)}) collective-permute-start(f32[2,384,4,128]{3,1,2,0:T(8,128)} %get-tuple-element.772), channel_id=1, source_target_pairs={{0,1},{1,2},{2,3},{3,4},{4,5},{5,6},{6,7},{7,8},{8,9},{9,10},{10,1... | collective-permute-start | bytes 4718600 | tf_op jit(solution)/shard_map/while/body/eval_jaxpr/ppermute | solution.py:118
  2369.0 144.2 %collective-permute-start.4 = (bf16[2,384,4,128]{3,1,2,0:T(8,128)(2,1)}, bf16[2,384,4,128]{3,1,2,0:T(8,128)(2,1)S(1)}, u32[]{:S(2)}, u32[]{:S(2)}) collective-permute-start(bf16[2,384,4,128]{3,1,2,0:T(8,128)(2,1)} %get-tuple-element.770), channel_id=1, source_target_pairs={{0,1},{1,2},{2,3},{3,4},{4,5},{5,6},{6,7},{7,8},{8,9},{9,10},{10,1... | collective-permute-start | bytes 2359304 | tf_op jit(solution)/shard_map/while/body/eval_jaxpr/ppermute | solution.py:116
  2519.5 145.8 %collective-permute-start.3 = (f32[2,384,4,128]{3,1,2,0:T(8,128)}, f32[2,384,4,128]{3,1,2,0:T(8,128)}, u32[]{:S(2)}, u32[]{:S(2)}) collective-permute-start(f32[2,384,4,128]{3,1,2,0:T(8,128)} %get-tuple-element.773), channel_id=1, source_target_pairs={{0,1},{1,2},{2,3},{3,4},{4,5},{5,6},{6,7},{7,8},{8,9},{9,10},{10,1... | collective-permute-start | bytes 4718600 | tf_op jit(solution)/shard_map/while/body/eval_jaxpr/ppermute | solution.py:119
  2519.5 145.8 %collective-permute-start.2 = (f32[2,384,4,128]{3,1,2,0:T(8,128)}, f32[2,384,4,128]{3,1,2,0:T(8,128)}, u32[]{:S(2)}, u32[]{:S(2)}) collective-permute-start(f32[2,384,4,128]{3,1,2,0:T(8,128)} %get-tuple-element.772), channel_id=1, source_target_pairs={{0,1},{1,2},{2,3},{3,4},{4,5},{5,6},{6,7},{7,8},{8,9},{9,10},{10,1... | collective-permute-start | bytes 4718600 | tf_op jit(solution)/shard_map/while/body/eval_jaxpr/ppermute | solution.py:118
  2519.6 136.4 %collective-permute-start.5 = (bf16[2,384,4,128]{3,1,2,0:T(8,128)(2,1)}, bf16[2,384,4,128]{3,1,2,0:T(8,128)(2,1)}, u32[]{:S(2)}, u32[]{:S(2)}) collective-permute-start(bf16[2,384,4,128]{3,1,2,0:T(8,128)(2,1)} %get-tuple-element.771), channel_id=1, source_target_pairs={{0,1},{1,2},{2,3},{3,4},{4,5},{5,6},{6,7},{7,8},{8,9},{9,10},{10,1... | collective-permute-start | bytes 2359304 | tf_op jit(solution)/shard_map/while/body/eval_jaxpr/ppermute | solution.py:117
  2520.1 144.2 %collective-permute-start.4 = (bf16[2,384,4,128]{3,1,2,0:T(8,128)(2,1)}, bf16[2,384,4,128]{3,1,2,0:T(8,128)(2,1)S(1)}, u32[]{:S(2)}, u32[]{:S(2)}) collective-permute-start(bf16[2,384,4,128]{3,1,2,0:T(8,128)(2,1)} %get-tuple-element.770), channel_id=1, source_target_pairs={{0,1},{1,2},{2,3},{3,4},{4,5},{5,6},{6,7},{7,8},{8,9},{9,10},{10,1... | collective-permute-start | bytes 2359304 | tf_op jit(solution)/shard_map/while/body/eval_jaxpr/ppermute | solution.py:116
  2670.7 145.8 %collective-permute-start.3 = (f32[2,384,4,128]{3,1,2,0:T(8,128)}, f32[2,384,4,128]{3,1,2,0:T(8,128)}, u32[]{:S(2)}, u32[]{:S(2)}) collective-permute-start(f32[2,384,4,128]{3,1,2,0:T(8,128)} %get-tuple-element.773), channel_id=1, source_target_pairs={{0,1},{1,2},{2,3},{3,4},{4,5},{5,6},{6,7},{7,8},{8,9},{9,10},{10,1... | collective-permute-start | bytes 4718600 | tf_op jit(solution)/shard_map/while/body/eval_jaxpr/ppermute | solution.py:119
  2670.7 145.8 %collective-permute-start.2 = (f32[2,384,4,128]{3,1,2,0:T(8,128)}, f32[2,384,4,128]{3,1,2,0:T(8,128)}, u32[]{:S(2)}, u32[]{:S(2)}) collective-permute-start(f32[2,384,4,128]{3,1,2,0:T(8,128)} %get-tuple-element.772), channel_id=1, source_target_pairs={{0,1},{1,2},{2,3},{3,4},{4,5},{5,6},{6,7},{7,8},{8,9},{9,10},{10,1... | collective-permute-start | bytes 4718600 | tf_op jit(solution)/shard_map/while/body/eval_jaxpr/ppermute | solution.py:118
  2671.3 144.2 %collective-permute-start.4 = (bf16[2,384,4,128]{3,1,2,0:T(8,128)(2,1)}, bf16[2,384,4,128]{3,1,2,0:T(8,128)(2,1)S(1)}, u32[]{:S(2)}, u32[]{:S(2)}) collective-permute-start(bf16[2,384,4,128]{3,1,2,0:T(8,128)(2,1)} %get-tuple-element.770), channel_id=1, source_target_pairs={{0,1},{1,2},{2,3},{3,4},{4,5},{5,6},{6,7},{7,8},{8,9},{9,10},{10,1... | collective-permute-start | bytes 2359304 | tf_op jit(solution)/shard_map/while/body/eval_jaxpr/ppermute | solution.py:116
  2821.8 145.8 %collective-permute-start.3 = (f32[2,384,4,128]{3,1,2,0:T(8,128)}, f32[2,384,4,128]{3,1,2,0:T(8,128)}, u32[]{:S(2)}, u32[]{:S(2)}) collective-permute-start(f32[2,384,4,128]{3,1,2,0:T(8,128)} %get-tuple-element.773), channel_id=1, source_target_pairs={{0,1},{1,2},{2,3},{3,4},{4,5},{5,6},{6,7},{7,8},{8,9},{9,10},{10,1... | collective-permute-start | bytes 4718600 | tf_op jit(solution)/shard_map/while/body/eval_jaxpr/ppermute | solution.py:119
  2821.9 145.8 %collective-permute-start.2 = (f32[2,384,4,128]{3,1,2,0:T(8,128)}, f32[2,384,4,128]{3,1,2,0:T(8,128)}, u32[]{:S(2)}, u32[]{:S(2)}) collective-permute-start(f32[2,384,4,128]{3,1,2,0:T(8,128)} %get-tuple-element.772), channel_id=1, source_target_pairs={{0,1},{1,2},{2,3},{3,4},{4,5},{5,6},{6,7},{7,8},{8,9},{9,10},{10,1... | collective-permute-start | bytes 4718600 | tf_op jit(solution)/shard_map/while/body/eval_jaxpr/ppermute | solution.py:118
  2821.9 136.4 %collective-permute-start.5 = (bf16[2,384,4,128]{3,1,2,0:T(8,128)(2,1)}, bf16[2,384,4,128]{3,1,2,0:T(8,128)(2,1)}, u32[]{:S(2)}, u32[]{:S(2)}) collective-permute-start(bf16[2,384,4,128]{3,1,2,0:T(8,128)(2,1)} %get-tuple-element.771), channel_id=1, source_target_pairs={{0,1},{1,2},{2,3},{3,4},{4,5},{5,6},{6,7},{7,8},{8,9},{9,10},{10,1... | collective-permute-start | bytes 2359304 | tf_op jit(solution)/shard_map/while/body/eval_jaxpr/ppermute | solution.py:117
  2822.5 144.2 %collective-permute-start.4 = (bf16[2,384,4,128]{3,1,2,0:T(8,128)(2,1)}, bf16[2,384,4,128]{3,1,2,0:T(8,128)(2,1)S(1)}, u32[]{:S(2)}, u32[]{:S(2)}) collective-permute-start(bf16[2,384,4,128]{3,1,2,0:T(8,128)(2,1)} %get-tuple-element.770), channel_id=1, source_target_pairs={{0,1},{1,2},{2,3},{3,4},{4,5},{5,6},{6,7},{7,8},{8,9},{9,10},{10,1... | collective-permute-start | bytes 2359304 | tf_op jit(solution)/shard_map/while/body/eval_jaxpr/ppermute | solution.py:116
  2973.0 145.8 %collective-permute-start.3 = (f32[2,384,4,128]{3,1,2,0:T(8,128)}, f32[2,384,4,128]{3,1,2,0:T(8,128)}, u32[]{:S(2)}, u32[]{:S(2)}) collective-permute-start(f32[2,384,4,128]{3,1,2,0:T(8,128)} %get-tuple-element.773), channel_id=1, source_target_pairs={{0,1},{1,2},{2,3},{3,4},{4,5},{5,6},{6,7},{7,8},{8,9},{9,10},{10,1... | collective-permute-start | bytes 4718600 | tf_op jit(solution)/shard_map/while/body/eval_jaxpr/ppermute | solution.py:119
  2973.0 145.8 %collective-permute-start.2 = (f32[2,384,4,128]{3,1,2,0:T(8,128)}, f32[2,384,4,128]{3,1,2,0:T(8,128)}, u32[]{:S(2)}, u32[]{:S(2)}) collective-permute-start(f32[2,384,4,128]{3,1,2,0:T(8,128)} %get-tuple-element.772), channel_id=1, source_target_pairs={{0,1},{1,2},{2,3},{3,4},{4,5},{5,6},{6,7},{7,8},{8,9},{9,10},{10,1... | collective-permute-start | bytes 4718600 | tf_op jit(solution)/shard_map/while/body/eval_jaxpr/ppermute | solution.py:118
  2973.7 144.2 %collective-permute-start.4 = (bf16[2,384,4,128]{3,1,2,0:T(8,128)(2,1)}, bf16[2,384,4,128]{3,1,2,0:T(8,128)(2,1)S(1)}, u32[]{:S(2)}, u32[]{:S(2)}) collective-permute-start(bf16[2,384,4,128]{3,1,2,0:T(8,128)(2,1)} %get-tuple-element.770), channel_id=1, source_target_pairs={{0,1},{1,2},{2,3},{3,4},{4,5},{5,6},{6,7},{7,8},{8,9},{9,10},{10,1... | collective-permute-start | bytes 2359304 | tf_op jit(solution)/shard_map/while/body/eval_jaxpr/ppermute | solution.py:116
  3124.2 145.8 %collective-permute-start.3 = (f32[2,384,4,128]{3,1,2,0:T(8,128)}, f32[2,384,4,128]{3,1,2,0:T(8,128)}, u32[]{:S(2)}, u32[]{:S(2)}) collective-permute-start(f32[2,384,4,128]{3,1,2,0:T(8,128)} %get-tuple-element.773), channel_id=1, source_target_pairs={{0,1},{1,2},{2,3},{3,4},{4,5},{5,6},{6,7},{7,8},{8,9},{9,10},{10,1... | collective-permute-start | bytes 4718600 | tf_op jit(solution)/shard_map/while/body/eval_jaxpr/ppermute | solution.py:119
  3124.2 145.8 %collective-permute-start.2 = (f32[2,384,4,128]{3,1,2,0:T(8,128)}, f32[2,384,4,128]{3,1,2,0:T(8,128)}, u32[]{:S(2)}, u32[]{:S(2)}) collective-permute-start(f32[2,384,4,128]{3,1,2,0:T(8,128)} %get-tuple-element.772), channel_id=1, source_target_pairs={{0,1},{1,2},{2,3},{3,4},{4,5},{5,6},{6,7},{7,8},{8,9},{9,10},{10,1... | collective-permute-start | bytes 4718600 | tf_op jit(solution)/shard_map/while/body/eval_jaxpr/ppermute | solution.py:118
  3124.3 136.4 %collective-permute-start.5 = (bf16[2,384,4,128]{3,1,2,0:T(8,128)(2,1)}, bf16[2,384,4,128]{3,1,2,0:T(8,128)(2,1)}, u32[]{:S(2)}, u32[]{:S(2)}) collective-permute-start(bf16[2,384,4,128]{3,1,2,0:T(8,128)(2,1)} %get-tuple-element.771), channel_id=1, source_target_pairs={{0,1},{1,2},{2,3},{3,4},{4,5},{5,6},{6,7},{7,8},{8,9},{9,10},{10,1... | collective-permute-start | bytes 2359304 | tf_op jit(solution)/shard_map/while/body/eval_jaxpr/ppermute | solution.py:117
  3124.8 144.2 %collective-permute-start.4 = (bf16[2,384,4,128]{3,1,2,0:T(8,128)(2,1)}, bf16[2,384,4,128]{3,1,2,0:T(8,128)(2,1)S(1)}, u32[]{:S(2)}, u32[]{:S(2)}) collective-permute-start(bf16[2,384,4,128]{3,1,2,0:T(8,128)(2,1)} %get-tuple-element.770), channel_id=1, source_target_pairs={{0,1},{1,2},{2,3},{3,4},{4,5},{5,6},{6,7},{7,8},{8,9},{9,10},{10,1... | collective-permute-start | bytes 2359304 | tf_op jit(solution)/shard_map/while/body/eval_jaxpr/ppermute | solution.py:116
  3275.4 145.8 %collective-permute-start.3 = (f32[2,384,4,128]{3,1,2,0:T(8,128)}, f32[2,384,4,128]{3,1,2,0:T(8,128)}, u32[]{:S(2)}, u32[]{:S(2)}) collective-permute-start(f32[2,384,4,128]{3,1,2,0:T(8,128)} %get-tuple-element.773), channel_id=1, source_target_pairs={{0,1},{1,2},{2,3},{3,4},{4,5},{5,6},{6,7},{7,8},{8,9},{9,10},{10,1... | collective-permute-start | bytes 4718600 | tf_op jit(solution)/shard_map/while/body/eval_jaxpr/ppermute | solution.py:119
  3275.4 145.8 %collective-permute-start.2 = (f32[2,384,4,128]{3,1,2,0:T(8,128)}, f32[2,384,4,128]{3,1,2,0:T(8,128)}, u32[]{:S(2)}, u32[]{:S(2)}) collective-permute-start(f32[2,384,4,128]{3,1,2,0:T(8,128)} %get-tuple-element.772), channel_id=1, source_target_pairs={{0,1},{1,2},{2,3},{3,4},{4,5},{5,6},{6,7},{7,8},{8,9},{9,10},{10,1... | collective-permute-start | bytes 4718600 | tf_op jit(solution)/shard_map/while/body/eval_jaxpr/ppermute | solution.py:118
  3276.0 144.2 %collective-permute-start.4 = (bf16[2,384,4,128]{3,1,2,0:T(8,128)(2,1)}, bf16[2,384,4,128]{3,1,2,0:T(8,128)(2,1)S(1)}, u32[]{:S(2)}, u32[]{:S(2)}) collective-permute-start(bf16[2,384,4,128]{3,1,2,0:T(8,128)(2,1)} %get-tuple-element.770), channel_id=1, source_target_pairs={{0,1},{1,2},{2,3},{3,4},{4,5},{5,6},{6,7},{7,8},{8,9},{9,10},{10,1... | collective-permute-start | bytes 2359304 | tf_op jit(solution)/shard_map/while/body/eval_jaxpr/ppermute | solution.py:116
  3426.5 145.8 %collective-permute-start.3 = (f32[2,384,4,128]{3,1,2,0:T(8,128)}, f32[2,384,4,128]{3,1,2,0:T(8,128)}, u32[]{:S(2)}, u32[]{:S(2)}) collective-permute-start(f32[2,384,4,128]{3,1,2,0:T(8,128)} %get-tuple-element.773), channel_id=1, source_target_pairs={{0,1},{1,2},{2,3},{3,4},{4,5},{5,6},{6,7},{7,8},{8,9},{9,10},{10,1... | collective-permute-start | bytes 4718600 | tf_op jit(solution)/shard_map/while/body/eval_jaxpr/ppermute | solution.py:119
  3426.6 145.8 %collective-permute-start.2 = (f32[2,384,4,128]{3,1,2,0:T(8,128)}, f32[2,384,4,128]{3,1,2,0:T(8,128)}, u32[]{:S(2)}, u32[]{:S(2)}) collective-permute-start(f32[2,384,4,128]{3,1,2,0:T(8,128)} %get-tuple-element.772), channel_id=1, source_target_pairs={{0,1},{1,2},{2,3},{3,4},{4,5},{5,6},{6,7},{7,8},{8,9},{9,10},{10,1... | collective-permute-start | bytes 4718600 | tf_op jit(solution)/shard_map/while/body/eval_jaxpr/ppermute | solution.py:118
  3427.2 144.2 %collective-permute-start.4 = (bf16[2,384,4,128]{3,1,2,0:T(8,128)(2,1)}, bf16[2,384,4,128]{3,1,2,0:T(8,128)(2,1)S(1)}, u32[]{:S(2)}, u32[]{:S(2)}) collective-permute-start(bf16[2,384,4,128]{3,1,2,0:T(8,128)(2,1)} %get-tuple-element.770), channel_id=1, source_target_pairs={{0,1},{1,2},{2,3},{3,4},{4,5},{5,6},{6,7},{7,8},{8,9},{9,10},{10,1... | collective-permute-start | bytes 2359304 | tf_op jit(solution)/shard_map/while/body/eval_jaxpr/ppermute | solution.py:116
  3577.7 145.8 %collective-permute-start.3 = (f32[2,384,4,128]{3,1,2,0:T(8,128)}, f32[2,384,4,128]{3,1,2,0:T(8,128)}, u32[]{:S(2)}, u32[]{:S(2)}) collective-permute-start(f32[2,384,4,128]{3,1,2,0:T(8,128)} %get-tuple-element.773), channel_id=1, source_target_pairs={{0,1},{1,2},{2,3},{3,4},{4,5},{5,6},{6,7},{7,8},{8,9},{9,10},{10,1... | collective-permute-start | bytes 4718600 | tf_op jit(solution)/shard_map/while/body/eval_jaxpr/ppermute | solution.py:119
  3577.7 145.8 %collective-permute-start.2 = (f32[2,384,4,128]{3,1,2,0:T(8,128)}, f32[2,384,4,128]{3,1,2,0:T(8,128)}, u32[]{:S(2)}, u32[]{:S(2)}) collective-permute-start(f32[2,384,4,128]{3,1,2,0:T(8,128)} %get-tuple-element.772), channel_id=1, source_target_pairs={{0,1},{1,2},{2,3},{3,4},{4,5},{5,6},{6,7},{7,8},{8,9},{9,10},{10,1... | collective-permute-start | bytes 4718600 | tf_op jit(solution)/shard_map/while/body/eval_jaxpr/ppermute | solution.py:118
  3578.4 144.2 %collective-permute-start.4 = (bf16[2,384,4,128]{3,1,2,0:T(8,128)(2,1)}, bf16[2,384,4,128]{3,1,2,0:T(8,128)(2,1)S(1)}, u32[]{:S(2)}, u32[]{:S(2)}) collective-permute-start(bf16[2,384,4,128]{3,1,2,0:T(8,128)(2,1)} %get-tuple-element.770), channel_id=1, source_target_pairs={{0,1},{1,2},{2,3},{3,4},{4,5},{5,6},{6,7},{7,8},{8,9},{9,10},{10,1... | collective-permute-start | bytes 2359304 | tf_op jit(solution)/shard_map/while/body/eval_jaxpr/ppermute | solution.py:116
  (125 other events, 5256.4 us)
Sparse Core Ops, SparseCore 0:
  3867.5 746.5 all-reduce.7
where the time goes:
time: 4680 us; the launch traced here: 4670 us
  waiting for transfers between devices  3640 us (78%)
  local copies, waits for them, and re-layouts  343 us (7%)
  matrix products  265 us (6%)
  other arithmetic  150 us (3%)
  starting transfers between devices  131 us (3%)
  blocking collectives  124 us (3%)
    ppermute x15, waiting for transfers between devices, bwd_step(): v_cur = lax.ppermute(v_cur, 'cp', next_perm)  2000 us
    ppermute x15, waiting for transfers between devices, fwd_step(): v_cur = lax.ppermute(v_cur, 'cp', next_perm)  847 us
    psum x1, waiting for transfers between devices, local_block(): lax.psum((wgrad_query, wgrad_key, wgrad_value, wgrad_out, ngrad_attn, ngr...  567 us
    while x150, local copies, waits for them, and re-layouts  177 us
    ppermute x15, waiting for transfers between devices, fwd_step(): k_cur = lax.ppermute(k_cur, 'cp', next_perm)  126 us
    psum x1, blocking collectives, local_block(): lax.psum((wgrad_query, wgrad_key, wgrad_value, wgrad_out, ngrad_attn, ngr...  124 us
    ppermute x15, waiting for transfers between devices, bwd_step(): k_cur = lax.ppermute(k_cur, 'cp', next_perm)  95.3 us
  transfers between devices with their start and end apart: 93, of which 61 were waited for; matrix products, arithmetic and copies ran while one was open for 5% of the time, Pallas kernels for 0%

commit v1 on v0

v1 whole, which is shorter than its diff:
```python
import functools
import math

import jax
import jax.numpy as jnp
from jax import lax
from jax.experimental import pallas as pl
from jax.experimental.pallas import tpu as pltpu
from jax.sharding import PartitionSpec as P


ROPE_THETA = 1000000.0
NORM_EPS = 1e-6
HEAD_DIM=128; F32=jnp.float32; BF16=jnp.bfloat16
SCALE = HEAD_DIM ** -0.5
EXP2_SCALE = SCALE * math.log2(math.e)
UR = 256


def nn(a, b): return lax.dot_general(a, b, (((1,), (0,)), ((), ())), preferred_element_type=F32)


def nt(a, b): return lax.dot_general(a, b, (((1,), (1,)), ((), ())), preferred_element_type=F32)


def lanes(i): return slice(i * HEAD_DIM, (i + 1) * HEAD_DIM)


def params(**more):
    return pltpu.CompilerParams(dimension_semantics=("arbitrary",), vmem_limit_bytes=60000000, **more)


def cost(flops, nbytes):
    return pl.CostEstimate(flops=flops, bytes_accessed=nbytes, transcendentals=0)


def whole(a):
    return pl.BlockSpec(a.shape, lambda t: (0,) * a.ndim)


def peers_of(kind, me):
    return [me ^ k for k in range(1, 16)] if kind == "all" else [me ^ {"pair": 2, "core": 1}[kind]]


def carrying(kernel, n_in, n_out, n_scratch, steps, kinds):
    if not kinds:
        return kernel
    m = len(kinds)

    def body(*refs):
        ins, srcs, refs = refs[:n_in], refs[n_in:n_in + m], refs[n_in + m:]
        outs, dsts, refs = refs[:n_out], refs[n_out:n_out + m], refs[n_out + m:]
        scratch, sems = refs[:n_scratch], refs[n_scratch:]
        step = pl.program_id(0)
        me = lax.axis_index('cp')

        def copies():
            made = []
            for i, kind in enumerate(kinds):
                send, recv, own = sems[3 * i:3 * i + 3]
                for n, peer in enumerate(peers_of(kind, me)):
                    src, dst = (srcs[i].at[peer], dsts[i].at[me]) if kind == "all" else (srcs[i], dsts[i])
                    made.append(pltpu.make_async_remote_copy(src_ref=src, dst_ref=dst, send_sem=send.at[n], recv_sem=recv.at[n],
                                                             device_id=(peer,), device_id_type=pl.DeviceIdType.MESH))
                if kind == "all":
                    made.append(pltpu.make_async_copy(srcs[i].at[me], dsts[i].at[me], own))
            return made

        @pl.when(step == 0)
        def _():
            barrier = pltpu.get_barrier_semaphore()
            flips = sorted({k for kind in kinds for k in (range(1, 16) if kind == "all" else [{"pair": 2, "core": 1}[kind]])})
            for k in flips:
                pl.semaphore_signal(barrier, inc=1, device_id=(me ^ k,), device_id_type=pl.DeviceIdType.MESH)
            pl.semaphore_wait(barrier, len(flips))
            for copy in copies():
                copy.start()

        kernel(*ins, *outs, *scratch)

        @pl.when(step == steps - 1)
        def _():
            for copy in copies():
                copy.wait()

    return body


def call(kernel, grid, in_specs, out_specs, out_shape, scratch, estimate, operands, carry=(), key=None):
    kinds = [kind for kind, _ in carry]
    hbm = pl.BlockSpec(memory_space=pltpu.HBM)
    sems = []
    for kind in kinds:
        count = 15 if kind == "all" else 1
        sems += [pltpu.SemaphoreType.DMA((count,)), pltpu.SemaphoreType.DMA((count,)), pltpu.SemaphoreType.DMA]
    more = dict(collective_id=key, has_side_effects=True) if kinds else {}
    return pl.pallas_call(
        carrying(kernel, len(operands), len(out_shape), len(scratch), grid, kinds), grid=(grid,),
        in_specs=list(in_specs) + [hbm] * len(kinds), out_specs=list(out_specs) + [hbm] * len(kinds),
        out_shape=list(out_shape) + [jax.ShapeDtypeStruct(a.shape, a.dtype) for _, a in carry],
        scratch_shapes=list(scratch) + sems, compiler_params=params(**more), cost_estimate=estimate,
    )(*operands, *[a for _, a in carry])


def key_mask(width):
    return lax.broadcasted_iota(jnp.int32, (UR, width), 0) + (width - UR) >= lax.broadcasted_iota(jnp.int32, (UR, width), 1)


def flash_fwd_kernel(nh, rh, tk, q_ref, kt_ref, v_ref, o_ref, lse_ref, s_ref, acc_ref, m_ref, l_ref):
    tile = pl.program_id(0)
    tq = rh * UR
    classes = tk // tq
    units = [(r, head) for r in range(rh) for head in range(nh)]
    m_ref[...] = jnp.full_like(m_ref, -jnp.inf)
    l_ref[...] = jnp.zeros_like(l_ref)
    acc_ref[...] = jnp.zeros_like(acc_ref)
    query = lambda u: q_ref[u[0] * UR:(u[0] + 1) * UR, lanes(u[1])]
    for n, u in enumerate(units):
        s_ref[n] = nn(query(u), kt_ref[:, :tk])

    def update(n, keys, scores, width):
        top = scores[:, :HEAD_DIM]
        for piece in range(1, width // HEAD_DIM):
            top = jnp.maximum(top, scores[:, lanes(piece)])
        m_prev = m_ref[n]
        m_new = jnp.maximum(m_prev, jnp.max(top, axis=-1, keepdims=True))
        alpha = jnp.exp2((m_prev - m_new) * EXP2_SCALE)
        shift = m_new * EXP2_SCALE
        part, pieces = None, []
        for piece in range(width // HEAD_DIM):
            prob = jnp.exp2(scores[:, lanes(piece)] * EXP2_SCALE - shift)
            part = prob if part is None else part + prob
            pieces.append(prob.astype(BF16))
        m_ref[n] = m_new
        l_ref[n] = l_ref[n] * alpha + part
        acc_ref[n] = acc_ref[n] * alpha + nn(jnp.concatenate(pieces, axis=1), v_ref[keys, :])

    last = tile // classes

    @pl.loop(0, last)
    def _(j):
        keys = pl.ds(pl.multiple_of(j * tk, tk), tk)
        following = pl.ds(pl.multiple_of(j * tk + tk, tk), tk)
        for n, u in enumerate(units):
            update(n, keys, s_ref[n], tk)
            s_ref[n] = nn(query(u), kt_ref[:, following])

    for c in range(classes):
        @pl.when(tile % classes == c)
        def _():
            for n, u in enumerate(units):
                width = c * tq + (u[0] + 1) * UR
                keys = pl.ds(pl.multiple_of(last * tk, tk), width)
                update(n, keys, jnp.where(key_mask(width), s_ref[n, :, :width], -jnp.inf), width)

    for n, u in enumerate(units):
        rows = slice(u[0] * UR, (u[0] + 1) * UR)
        total = jnp.sum(l_ref[n], axis=-1, keepdims=True)
        o_ref[rows, lanes(u[1])] = (acc_ref[n] / total).astype(BF16)
        lse_ref[rows, lanes(u[1])] = m_ref[n] * EXP2_SCALE + jnp.log2(total)


def run_fwd(q, kt, v, chunk, nh, rh, tk, carry=(), key=None):
    seq, width, tq = q.shape[0], nh * HEAD_DIM, rh * UR
    out = pl.BlockSpec((tq, width), lambda t: (t, 0))
    stat = pltpu.VMEM((nh * rh, UR, HEAD_DIM), F32)
    sds = jax.ShapeDtypeStruct
    return call(functools.partial(flash_fwd_kernel, nh, rh, tk), seq // tq,
                [pl.BlockSpec((tq, width), lambda t: (t, chunk)), whole(kt), whole(v)], [out, out], [sds((seq, width), BF16), sds((seq, width), F32)],
                [pltpu.VMEM((nh * rh, UR, tk), F32), stat, stat, stat], cost(2 * seq * seq * width, seq * 4096), (q, kt, v), carry, key)


def flash_bwd_kernel(nh, rh, tk, q_ref, do_ref, o_ref, lse_ref, kt_ref, vt_ref, k_ref, dq_ref, dkt_ref, dvt_ref, acc_ref, qt_ref, dot_ref, delta_ref, p_ref, ds_ref):
    tile = pl.program_id(0)
    tq = rh * UR
    classes = tk // tq
    units = [(r, head) for r in range(rh) for head in range(nh)]
    rows_of = lambda u: slice(u[0] * UR, (u[0] + 1) * UR)
    at = lambda n: slice(n * UR, (n + 1) * UR)

    @pl.when(tile == 0)
    def _():
        dkt_ref[...] = jnp.zeros_like(dkt_ref)
        dvt_ref[...] = jnp.zeros_like(dvt_ref)

    acc_ref[...] = jnp.zeros_like(acc_ref)
    for n, u in enumerate(units):
        qt_ref[:, at(n)] = q_ref[rows_of(u), lanes(u[1])].astype(F32).T.astype(BF16)
        do = do_ref[rows_of(u), lanes(u[1])].astype(F32)
        dot_ref[:, at(n)] = do.T.astype(BF16)
        delta = jnp.sum(do * o_ref[rows_of(u), lanes(u[1])].astype(F32), axis=-1, keepdims=True)
        delta_ref[n] = jnp.broadcast_to(delta, (UR, HEAD_DIM))

    def unit(n, u, keys, width, masked):
        scores = nn(q_ref[rows_of(u), lanes(u[1])], kt_ref[:, keys])
        if masked:
            scores = jnp.where(key_mask(width), scores, -jnp.inf)
        d_prob = nn(do_ref[rows_of(u), lanes(u[1])], vt_ref[:, keys])
        lse, delta = lse_ref[rows_of(u), lanes(u[1])], delta_ref[n]
        for piece in range(width // HEAD_DIM):
            prob = jnp.exp2(scores[:, lanes(piece)] * EXP2_SCALE - lse)
            p_ref[at(n), lanes(piece)] = prob.astype(BF16)
            ds_ref[at(n), lanes(piece)] = (prob * (d_prob[:, lanes(piece)] - delta)).astype(BF16)

    def products(rows, keys, width):
        dvt_ref[:, keys] += nn(dot_ref[:, rows], p_ref[rows, :width])
        dkt_ref[:, keys] += nn(qt_ref[:, rows], ds_ref[rows, :width])
        acc_ref[rows, :] += nn(ds_ref[rows, :width], k_ref[keys, :])

    last = tile // classes

    @pl.loop(0, last)
    def _(j):
        keys = pl.ds(pl.multiple_of(j * tk, tk), tk)
        for n, u in enumerate(units):
            unit(n, u, keys, tk, False)
        products(slice(0, len(units) * UR), keys, tk)

    for c in range(classes):
        @pl.when(tile % classes == c)
        def _():
            for r in range(rh):
                width = c * tq + (r + 1) * UR
                keys = pl.ds(pl.multiple_of(last * tk, tk), width)
                for n, u in enumerate(units):
                    if u[0] == r:
                        unit(n, u, keys, width, True)
                products(slice(r * nh * UR, (r + 1) * nh * UR), keys, width)

    for n, u in enumerate(units):
        dq_ref[rows_of(u), lanes(u[1])] = (acc_ref[at(n), :] * SCALE).astype(BF16)

    @pl.when(tile == pl.num_programs(0) - 1)
    def _():
        dkt_ref[...] = dkt_ref[...] * SCALE


def run_bwd(q, do, o, lse, kt, vt, k, chunk, nh, rh, tk, carry=(), key=None):
    seq, width, tq, rows = q.shape[0], nh * HEAD_DIM, rh * UR, nh * rh * UR
    row = pl.BlockSpec((tq, width), lambda t: (t, 0))
    sds = jax.ShapeDtypeStruct
    return call(functools.partial(flash_bwd_kernel, nh, rh, tk), seq // tq,
                [pl.BlockSpec((tq, width), lambda t: (t, chunk)), row, row, row, whole(kt), whole(vt), whole(k)], [row, whole(kt), whole(kt)],
                [sds((seq, width), BF16), sds(kt.shape, F32), sds(kt.shape, F32)],
                [pltpu.VMEM((rows, HEAD_DIM), F32), pltpu.VMEM((HEAD_DIM, rows), BF16), pltpu.VMEM((HEAD_DIM, rows), BF16),
                 pltpu.VMEM((nh * rh, UR, HEAD_DIM), F32), pltpu.VMEM((rows, tk), BF16), pltpu.VMEM((rows, tk), BF16)],
                cost(5 * seq * seq * width, seq * 8192), (q, do, o, lse, kt, vt, k), carry, key)


def tn(a, b):
    return nn(a.astype(F32).T.astype(BF16), b)


def rope_tables(offset, length):
    inv_freq = ROPE_THETA ** (-jnp.arange(0, HEAD_DIM, 2, dtype=F32) / HEAD_DIM)
    angles = (offset + jnp.arange(length)).astype(F32)[:, None] * inv_freq[None, :]
    cos_t, sin_t = jnp.cos(angles), jnp.sin(angles)
    return jnp.concatenate([cos_t, cos_t], axis=-1), jnp.concatenate([-sin_t, sin_t], axis=-1)


def half_roll(x):
    return pltpu.roll(x, HEAD_DIM // 2, 1)


def head_finish(pre, gain, cos_t, sin_t):
    scale = lax.rsqrt(jnp.mean(pre * pre, axis=-1, keepdims=True) + NORM_EPS)
    normed = pre * scale * gain
    return normed * cos_t + half_roll(normed) * sin_t


def head_finish_bwd(pre, gain, cos_t, sin_t, d_rot):
    d_normed = d_rot * cos_t - half_roll(d_rot) * sin_t
    scale = lax.rsqrt(jnp.mean(pre * pre, axis=-1, keepdims=True) + NORM_EPS)
    unit = pre * scale
    d_unit = d_normed * gain
    return scale * (d_unit - unit * jnp.mean(d_unit * unit, axis=-1, keepdims=True)), d_normed * unit


def slot_of(tok):
    return ((tok // 4) * 2 + tok % 2) * 2 + (tok // 2) % 2


def qkv_kernel(x_ref, gain_ref, w_ref, qn_ref, kn_ref, cos_ref, sin_ref, h_ref, qpre_ref, kpre_ref, q_ref, k_ref, kt_ref, v_ref, vt_ref):
    rows = x_ref.shape[1]
    step = rows // 3
    for first in range(0, rows, step):
        rs = slice(first, first + step)
        x = x_ref[0, rs].astype(F32)
        scale = lax.rsqrt(jnp.mean(x * x, axis=-1, keepdims=True) + NORM_EPS)
        h = (x * scale * gain_ref[...]).astype(BF16)
        h_ref[rs] = h
        pre = nn(h, w_ref[...])
        cos_t, sin_t = cos_ref[rs], sin_ref[rs]
        qpre_ref[rs] = pre[:, :4 * HEAD_DIM]
        for head in range(4):
            q_ref[rs, lanes(head)] = head_finish(pre[:, lanes(head)], qn_ref[...], cos_t, sin_t).astype(BF16)
        kpre = pre[:, lanes(4)]
        kpre_ref[rs] = kpre
        k_rot = head_finish(kpre, kn_ref[...], cos_t, sin_t)
        k_ref[rs] = k_rot.astype(BF16)
        kt_ref[:, rs] = k_rot.T.astype(BF16)
        v = pre[:, lanes(5)]
        v_ref[rs] = v.astype(BF16)
        vt_ref[:, rs] = v.T.astype(BF16)


def run_qkv(xg, gain, w_all, qn, kn, cos_t, sin_t):
    blocks, rows, dim = xg.shape
    seq = blocks * rows
    row = lambda width: pl.BlockSpec((rows, width), lambda t: (t, 0))
    col = pl.BlockSpec((HEAD_DIM, rows), lambda t: (0, t))
    sds = jax.ShapeDtypeStruct
    return pl.pallas_call(
        qkv_kernel, grid=(blocks,), name="qkv",
        in_specs=[pl.BlockSpec((1, rows, dim), lambda t: (slot_of(t), 0, 0)), whole(gain), whole(w_all), whole(qn), whole(kn), row(HEAD_DIM), row(HEAD_DIM)],
        out_specs=[row(dim), row(4 * HEAD_DIM), row(HEAD_DIM), row(4 * HEAD_DIM), row(HEAD_DIM), col, row(HEAD_DIM), col],
        out_shape=[sds((seq, dim), BF16), sds((seq, 4 * HEAD_DIM), F32), sds((seq, HEAD_DIM), F32), sds((seq, 4 * HEAD_DIM), BF16),
                   sds((seq, HEAD_DIM), BF16), sds((HEAD_DIM, seq), BF16), sds((seq, HEAD_DIM), BF16), sds((HEAD_DIM, seq), BF16)],
        compiler_params=params(), cost_estimate=cost(2 * seq * dim * 768, seq * dim * 8),
    )(xg, gain, w_all, qn, kn, cos_t, sin_t)


def out_grad_kernel(g_ref, w_ref, o_ref, do_ref, wg_ref):
    g = g_ref[0]
    do_ref[...] = nn(g, w_ref[...]).astype(BF16)

    @pl.when(pl.program_id(0) == 0)
    def _():
        wg_ref[...] = jnp.zeros_like(wg_ref)

    wg_ref[...] += tn(o_ref[...], g)


def run_out_grad(gg, wo, o):
    blocks, rows, dim = gg.shape
    width = wo.shape[1]
    row = pl.BlockSpec((rows, width), lambda t: (t, 0))
    return pl.pallas_call(
        out_grad_kernel, grid=(blocks,), name="out_grad",
        in_specs=[pl.BlockSpec((1, rows, dim), lambda t: (slot_of(t), 0, 0)), whole(wo), row], out_specs=[row, pl.BlockSpec((width, dim), lambda t: (0, 0))],
        out_shape=[jax.ShapeDtypeStruct(o.shape, BF16), jax.ShapeDtypeStruct((width, dim), F32)],
        compiler_params=params(), cost_estimate=cost(4 * blocks * rows * dim * width, blocks * rows * dim * 2),
    )(gg, wo, o)


def in_grad_kernel(with_kv, *refs):
    if with_kv:
        dq_ref, qpre_ref, qn_ref, cos_ref, sin_ref, h_ref, kv_ref, kpre_ref, kn_ref, half_ref, wg_ref, kvb_ref, dt_ref = refs
    else:
        dq_ref, qpre_ref, qn_ref, cos_ref, sin_ref, h_ref, wg_ref, dt_ref = refs

    @pl.when(pl.program_id(0) == 0)
    def _():
        wg_ref[...] = jnp.zeros_like(wg_ref)
        dt_ref[...] = jnp.zeros_like(dt_ref)

    wg_ref[...] += nn(dt_ref[...], h_ref[...])
    cos_t, sin_t = cos_ref[...], sin_ref[...]
    for head in range(2):
        d_pre, _ = head_finish_bwd(qpre_ref[:, lanes(head)], qn_ref[...], cos_t, sin_t, dq_ref[:, lanes(head)].astype(F32))
        dt_ref[lanes(head), :] = d_pre.T.astype(BF16)
    if with_kv:
        kv = kv_ref[...].T.astype(BF16)
        kvb_ref[...] = kv
        dk_pre, _ = head_finish_bwd(kpre_ref[...], kn_ref[...], cos_t, sin_t, kv.astype(F32))
        dt_ref[lanes(2), :] = jnp.where(half_ref[0] == 0, dk_pre, kv.astype(F32)).T.astype(BF16)


def run_in_grad(dq, qpre, chunk, qn, cos_t, sin_t, h, kv=None, carry=(), key=None):
    seq, dim = h.shape
    rows = 512
    count = seq // rows
    row = lambda width, c=0: pl.BlockSpec((rows, width), lambda t: (jnp.minimum(t, count - 1), c))
    operands = [dq, qpre, qn, cos_t, sin_t, h]
    specs = [row(256), row(256, chunk), whole(qn), row(HEAD_DIM), row(HEAD_DIM), pl.BlockSpec((rows, dim), lambda t: (jnp.maximum(t - 1, 0), 0))]
    height = 256
    out_specs, out_shape = [], []
    if kv is not None:
        kv_sum, kpre, kn, half = kv
        operands += [kv_sum, kpre, kn, half]
        specs += [pl.BlockSpec((HEAD_DIM, rows), lambda t: (0, jnp.minimum(t, count - 1))), row(HEAD_DIM), whole(kn), pl.BlockSpec(memory_space=pltpu.SMEM)]
        height = 384
        out_specs, out_shape = [row(HEAD_DIM)], [jax.ShapeDtypeStruct((seq, HEAD_DIM), BF16)]
    return call(functools.partial(in_grad_kernel, kv is not None), count + 1, specs, [pl.BlockSpec((height, dim), lambda t: (0, 0))] + out_specs,
                [jax.ShapeDtypeStruct((height, dim), F32)] + out_shape, [pltpu.VMEM((height, rows), BF16)], cost(2 * seq * dim * height, seq * dim * 3), operands, carry, key)


def out_proj_kernel(o0_ref, o1_ref, wa_ref, wb_ref, x_ref, y_ref, acc_ref):
    step = pl.program_id(0)

    @pl.when(step == 0)
    def _():
        acc_ref[...] = jnp.zeros_like(acc_ref)

    rows = x_ref.shape[1]
    o0, o1 = o0_ref[0, :, 0].reshape(2 * rows, 256), o1_ref[0, :, 0].reshape(2 * rows, 256)
    for j, w_ref in ((0, wa_ref), (1, wb_ref)):
        pair = jnp.concatenate([o0[:, lanes(j)], o1[:, lanes(j)]], axis=1)
        acc_ref[...] += nn(pair, w_ref[...])

    @pl.when(step == pl.num_programs(0) - 1)
    def _():
        for b in range(2):
            y_ref[b] = (x_ref[b].astype(F32) + acc_ref[b * rows:(b + 1) * rows, :]).astype(BF16)


def run_out_proj(o_got, w_out, hidden_in, carry=(), key=None):
    batch, rows, dim = hidden_in.shape
    src = pl.BlockSpec((1, 2, 1, rows, 256), lambda s: (s // 2, 0, s % 2, 0, 0))
    w_spec = lambda j: pl.BlockSpec((256, dim), lambda s: (4 * (s // 2) + 2 * j + s % 2, 0))
    return call(out_proj_kernel, 8, [src, src, w_spec(0), w_spec(1), whole(hidden_in)], [whole(hidden_in)],
                [jax.ShapeDtypeStruct(hidden_in.shape, BF16)], [pltpu.VMEM((batch * rows, dim), F32)],
                cost(2 * batch * rows * dim * 4096, 30000000), (o_got[0], o_got[1], w_out, w_out, hidden_in), carry, key)


def hidden_grad_kernel(dq0_ref, dq1_ref, kv_ref, qa_ref, qb_ref, kpre_ref, wqa_ref, wqb_ref, wk_ref, wv_ref, qn_ref, kn_ref, gain_ref,
                       cos_ref, sin_ref, x_ref, g_ref, dx_ref, ngq_ref, ngk_ref, ngx_ref, acc_ref):
    step = pl.program_id(0)
    rows = x_ref.shape[1]

    @pl.when(step == 0)
    def _():
        acc_ref[...] = jnp.zeros_like(acc_ref)
        ngq_ref[...] = jnp.zeros_like(ngq_ref)
        ngk_ref[...] = jnp.zeros_like(ngk_ref)

    is_key = step % 2 == 0
    cos_t = jnp.concatenate([cos_ref[...]] * 2, axis=0)
    sin_t = jnp.concatenate([sin_ref[...]] * 2, axis=0)
    dq0, dq1 = dq0_ref[0, :, 0].reshape(2 * rows, 256), dq1_ref[0, :, 0].reshape(2 * rows, 256)
    total = None
    for j, (q_ref, w_ref) in enumerate(((qa_ref, wqa_ref), (qb_ref, wqb_ref))):
        parts = []
        for c, dq in ((0, dq0), (1, dq1)):
            d_pre, terms = head_finish_bwd(q_ref[:, lanes(c)], qn_ref[...], cos_t, sin_t, dq[:, lanes(j)].astype(F32))
            parts.append(d_pre.astype(BF16))
            ngq_ref[...] += jnp.sum(terms.reshape(-1, 8, HEAD_DIM), axis=0)
        part = nt(jnp.concatenate(parts, axis=1), w_ref[...])
        total = part if total is None else total + part
    kv = kv_ref[0, :, 0].reshape(2 * rows, HEAD_DIM).astype(F32)
    dk_pre, terms = head_finish_bwd(kpre_ref[...], kn_ref[...], cos_t, sin_t, kv)
    ngk_ref[...] += jnp.where(is_key, jnp.sum(terms.reshape(-1, 8, HEAD_DIM), axis=0), 0.0)
    w_kv = jnp.where(is_key, wk_ref[...].astype(F32), wv_ref[...].astype(F32)).astype(BF16)
    acc_ref[...] += total + nt(jnp.where(is_key, dk_pre, kv).astype(BF16), w_kv)

    @pl.when(step == pl.num_programs(0) - 1)
    def _():
        partial = None
        for b in range(2):
            for r in range(0, rows, 64):
                rs = slice(r, r + 64)
                x = x_ref[b, rs].astype(F32)
                scale = lax.rsqrt(jnp.mean(x * x, axis=-1, keepdims=True) + NORM_EPS)
                unit = x * scale
                d_normed = acc_ref[b * rows + r:b * rows + r + 64, :].astype(BF16).astype(F32)
                terms = jnp.sum((d_normed * unit).reshape(8, 8, x.shape[1]), axis=0)
                partial = terms if partial is None else partial + terms
                d_unit = d_normed * gain_ref[...]
                d_x = scale * (d_unit - unit * jnp.mean(d_unit * unit, axis=-1, keepdims=True))
                dx_ref[b, rs] = (g_ref[b, rs].astype(F32) + d_x).astype(BF16)
        ngx_ref[...] = partial


def run_hidden_grad(dq_got, kv_got, qpre_own, kpre_own, w_query, w_key, w_value, qn, kn, gain, cos_t, sin_t, hidden_in, grad_out):
    batch, rows, dim = hidden_in.shape
    src = lambda width: pl.BlockSpec((1, 2, 1, rows, width), lambda s: (s // 2, 0, s % 2, 0, 0))
    cols = lambda height, j: pl.BlockSpec((height, 256), lambda s: (0, 4 * (s // 2) + 2 * j + s % 2))
    group = lambda height: pl.BlockSpec((height, HEAD_DIM), lambda s: (0, s // 2))
    fixed = lambda *shape: pl.BlockSpec(shape, lambda s: (0,) * len(shape))
    sds = jax.ShapeDtypeStruct
    both = batch * rows
    return pl.pallas_call(
        hidden_grad_kernel, grid=(8,), name="hidden_grad",
        in_specs=[src(256), src(256), src(HEAD_DIM), cols(both, 0), cols(both, 1), group(both), cols(dim, 0), cols(dim, 1), group(dim), group(dim),
                  whole(qn), whole(kn), whole(gain), whole(cos_t), whole(sin_t), whole(hidden_in), whole(grad_out)],
        out_specs=[whole(hidden_in), fixed(8, HEAD_DIM), fixed(8, HEAD_DIM), fixed(8, dim)],
        out_shape=[sds(hidden_in.shape, BF16), sds((8, HEAD_DIM), F32), sds((8, HEAD_DIM), F32), sds((8, dim), F32)],
        scratch_shapes=[pltpu.VMEM((both, dim), F32)],
        compiler_params=params(), cost_estimate=cost(2 * both * dim * 5120, 50000000),
    )(dq_got[0], dq_got[1], kv_got, qpre_own, qpre_own, kpre_own, w_query, w_query, w_key, w_value, qn, kn, gain, cos_t, sin_t, hidden_in, grad_out)


def place_kernel(*refs):
    refs[-1][...] = refs[0][0].T


def run_place(a, chunk, into=None):
    count, height, dim = a.shape[0], HEAD_DIM, a.shape[2]
    more = [] if into is None else [into]
    return pl.pallas_call(
        place_kernel, grid=(count,), name="place",
        in_specs=[pl.BlockSpec((1, height, dim), lambda t: (t, 0, 0))] + [pl.BlockSpec(memory_space=pltpu.HBM)] * len(more),
        out_specs=pl.BlockSpec((dim, height), lambda t: (0, 2 * t + chunk)), input_output_aliases={} if into is None else {1: 0},
        out_shape=jax.ShapeDtypeStruct((dim, 2 * height * count), F32), compiler_params=params(), cost_estimate=cost(1000000, 35000000),
    )(a, *more)


def solution(mesh):
    n_dev = mesh.shape['cp']
    seq_spec, rep_spec = P(None, 'cp', None), P()
    flip = lambda bit: [(dev, dev ^ bit) for dev in range(n_dev)]
    halves = [[dev for dev in range(n_dev) if (dev >> 1) & 1 == bit] for bit in (0, 1)]

    def local_block(hidden_in, grad_out, w_query, w_key, w_value, w_out, attn_norm, query_norm, key_norm):
        batch, seq_dev, dim = hidden_in.shape
        seq = seq_dev * n_dev
        kv_heads = w_key.shape[1] // HEAD_DIM
        me = lax.axis_index('cp')
        group, which, half = me // 4, (me // 2) % 2, me % 2
        gain = attn_norm.astype(F32).reshape(1, dim)
        qn, kn = query_norm.astype(F32).reshape(1, HEAD_DIM), key_norm.astype(F32).reshape(1, HEAD_DIM)

        gather_all = lambda x: lax.all_gather(x, 'cp')

        def gather_sequence(local):
            other = lax.dynamic_index_in_dim(local, 1 - which, 0, keepdims=False)
            got = lax.ppermute(other, 'cp', flip(2))
            pair = lax.dynamic_update_index_in_dim(local, got, 1 - which, 0)
            return lax.all_gather(pair, 'cp', axis_index_groups=halves, tiled=True)

        def split(parts):
            keep = lax.dynamic_index_in_dim(parts, which, 0, keepdims=False)
            return keep, lax.dynamic_index_in_dim(parts, 1 - which, 0, keepdims=False)

        blocks = lambda x: x.reshape(n_dev, seq_dev, x.shape[1])
        by_source = lambda x: x.reshape(4, 2, 2, seq_dev, x.shape[2])

        xg = gather_sequence(hidden_in)
        gg = gather_sequence(grad_out)
        cos_t, sin_t = rope_tables(0, seq)

        hidden = hidden_in.astype(F32)
        x_scale = lax.rsqrt(jnp.mean(hidden * hidden, axis=-1, keepdims=True) + NORM_EPS)
        h_own = (hidden * x_scale * gain).astype(BF16).reshape(batch * seq_dev, dim)
        qpre_own = nn(h_own, w_query)
        kpre_own = nn(h_own, w_key)

        head_at = lambda c, j: (8 * group + 4 * j + 2 * half + c) * HEAD_DIM
        order = [(c, j) for c in range(2) for j in range(2)]
        wq_mine = [lax.dynamic_slice_in_dim(w_query, head_at(c, j), HEAD_DIM, 1) for c, j in order]
        wk_mine = lax.dynamic_slice_in_dim(w_key, group * HEAD_DIM, HEAD_DIM, 1)
        wv_mine = lax.dynamic_slice_in_dim(w_value, group * HEAD_DIM, HEAD_DIM, 1)
        w_all = jnp.concatenate(wq_mine + [wk_mine, wv_mine], axis=1)
        wo_mine = [jnp.concatenate([lax.dynamic_slice_in_dim(w_out, head_at(c, j), HEAD_DIM, 0) for j in range(2)], axis=0).T for c in range(2)]

        xg, qpre_own, kpre_own = lax.optimization_barrier((xg, qpre_own, kpre_own))
        h, qpre, kpre, q, k, kt, v, vt = run_qkv(xg, gain, w_all, qn, kn, cos_t, sin_t)

        o0, lse0 = run_fwd(q, kt, v, 0, 2, 2, 1024)
        do0, wg_c = run_out_grad(gg, wo_mine[0], o0)
        keep, give = split(wg_c.reshape(2, HEAD_DIM, dim))
        o1, lse1, o_got0, got = run_fwd(q, kt, v, 1, 2, 2, 1024, [("all", blocks(o0)), ("pair", give)], 1)
        mine, o1 = lax.optimization_barrier((keep + got, o1))
        wg_out0 = gather_all(mine)
        do1, wg_c = run_out_grad(gg, wo_mine[1], o1)
        keep, give = split(wg_c.reshape(2, HEAD_DIM, dim))
        dq0, dkt0, dvt0, o_got1, got = run_bwd(q, do0, o0, lse0, kt, vt, k, 0, 2, 2, 1024, [("all", blocks(o1)), ("pair", give)], 2)
        mine, dq0 = lax.optimization_barrier((keep + got, dq0))
        wg_out1 = gather_all(mine)
        wgrad_out = jnp.stack([wg_out0, wg_out1], axis=1).reshape(w_out.shape)

        wg_c, = run_in_grad(dq0, qpre, 0, qn, cos_t, sin_t, h)
        keep, give = split(wg_c.reshape(2, HEAD_DIM, dim))
        dq1, dkt1, dvt1, dq_got0, got = run_bwd(q, do1, o1, lse1, kt, vt, k, 1, 2, 2, 1024, [("all", blocks(dq0)), ("pair", give)], 3)
        mine, dq1 = lax.optimization_barrier((keep + got, dq1))
        wg_q0 = gather_all(mine)
        dkt, dvt = dkt0 + dkt1, dvt0 + dvt1
        kv_keep, kv_give = jnp.where(half == 0, dkt, dvt), jnp.where(half == 0, dvt, dkt)
        kv_sum = kv_keep + lax.ppermute(kv_give, 'cp', flip(1))
        half_arr = half.astype(jnp.int32).reshape(1)
        wg_c, kv_b, dq_got1 = run_in_grad(dq1, qpre, 1, qn, cos_t, sin_t, h, (kv_sum, kpre, kn, half_arr), [("all", blocks(dq1))], 4)
        keep, give = split(jnp.concatenate([wg_c[:256].reshape(2, HEAD_DIM, dim), wg_c[256:].reshape(2, HEAD_DIM // 2, dim)], axis=1))
        hidden_out, kv_got, got = run_out_proj([by_source(o_got0), by_source(o_got1)], w_out, hidden_in, [("all", blocks(kv_b)), ("pair", give)], 5)
        mine, qpre_own = lax.optimization_barrier((keep + got, qpre_own))
        wg_q1 = gather_all(mine)
        wgrad_q = run_place(wg_q1, 1, run_place(wg_q0, 0))
        wg_kv = wg_q1[:, HEAD_DIM:].reshape(4, 2, 2, HEAD_DIM // 2, dim).transpose(2, 4, 0, 1, 3).reshape(2, dim, kv_heads * HEAD_DIM)
        dq_got, kv_got = [by_source(dq_got0), by_source(dq_got1)], by_source(kv_got)

        my_cos, my_sin = rope_tables(me * seq_dev, seq_dev)
        grad_in, ng_q, ng_k, ng_x = run_hidden_grad(dq_got, kv_got, qpre_own, kpre_own, w_query, w_key, w_value, qn, kn, gain, my_cos, my_sin, hidden_in, grad_out)
        norms = jnp.concatenate([jnp.sum(ng_x, axis=0), jnp.sum(ng_q, axis=0), jnp.sum(ng_k, axis=0)])
        norms = lax.psum(norms, 'cp')
        return (hidden_out, grad_in, wgrad_q, wg_kv[0], wg_kv[1], wgrad_out,
                norms[:dim], norms[dim:dim + HEAD_DIM], norms[dim + HEAD_DIM:])

    return jax.shard_map(local_block, mesh=mesh, in_specs=(seq_spec, seq_spec) + (rep_spec,) * 7, out_specs=(seq_spec, seq_spec) + (rep_spec,) * 7, check_vma=False)
```

time: 4680 us -> 1100 us (0.24)
  waiting for transfers between devices: 3640 us -> 90 us
  Pallas kernels: 0 us -> 781 us
  local copies, waits for them, and re-layouts: 343 us -> 81.7 us
  matrix products: 265 us -> 20.3 us
  starting transfers between devices: 131 us -> 5.53 us
  blocking collectives: 124 us -> 33.4 us
  other arithmetic: 150 us -> 63.4 us
    ppermute x92 -> x3, waiting for transfers between devices: 3070 us -> 73.6 us  [the longest x2 68.2 us: gather_sequence(): got = lax.ppermute(other, 'cp', flip(2))]
    pallas_call x0 -> x13, Pallas kernels: none -> 781 us  [the longest x7 570 us: call(): pl.pallas_call(carrying(kernel, len(operands), len(out_shape), len(scratc...]
    psum x1 -> x0, waiting for transfers between devices: 567 us -> none  [local_block(): lax.psum((wgrad_query, wgrad_key, wgrad_value, wgrad_out, ngrad_attn, ngr...]
    dot_general x18 -> x2, matrix products: 265 us -> 20.3 us  [nn(): lax.dot_general(a, b, (((1,), (0,)), ((), ())), preferred_element_type=F32)]
    while x158 -> x0, local copies, waits for them, and re-layouts: 212 us -> none
    ppermute x92 -> x3, starting transfers between devices: 131 us -> 5.29 us  [the longest x2 5.01 us: gather_sequence(): got = lax.ppermute(other, 'cp', flip(2))]
    psum x1, blocking collectives: 124 us -> 33.4 us  [local_block(): norms = lax.psum(norms, 'cp')]
    reduce_sum x6 -> x4, other arithmetic: 52.5 us -> 2.93 us  [the longest x1 0.86 us: local_block(): jnp.sum(ng_x, axis=0)]
  transfers between devices with their start and end apart: 93 -> 9, of which waited for: 61 -> 5; matrix products, arithmetic and copies ran while one was open for 5% -> 11% of each run, Pallas kernels for 0% -> 45%
where the time goes in v1:
time: 1100 us; the launch traced here: 1090 us
  Pallas kernels  781 us (71%)
  waiting for transfers between devices  90 us (8%)
  local copies, waits for them, and re-layouts  81.7 us (7%)
  other arithmetic  63.4 us (6%)
  blocking collectives  33.4 us (3%)
  matrix products  20.3 us (2%)
  between operations  15.1 us (1%)
    pallas_call x7, Pallas kernels, call(): pl.pallas_call(carrying(kernel, len(operands), len(out_shape), len(scratc...  570 us
    pallas_call x2, Pallas kernels, run_out_grad(): pl.pallas_call(out_grad_kernel, grid=(blocks,), name='out_grad', in_specs...  76.4 us
    ppermute x2, waiting for transfers between devices, gather_sequence(): got = lax.ppermute(other, 'cp', flip(2))  68.2 us
    pallas_call x1, Pallas kernels, run_hidden_grad(): pl.pallas_call(hidden_grad_kernel, grid=(8,), name='hidden_grad', in_spec...  54.5 us
    pallas_call x1, Pallas kernels, run_qkv(): pl.pallas_call(qkv_kernel, grid=(blocks,), name='qkv', in_specs=[pl.Block...  41.2 us
    pallas_call x2, Pallas kernels, run_place(): pl.pallas_call(place_kernel, grid=(count,), name='place', in_specs=[pl.Bl...  38.3 us
    unnamed x70, local copies, waits for them, and re-layouts  35.3 us
    psum x1, blocking collectives, local_block(): norms = lax.psum(norms, 'cp')  33.4 us
  transfers between devices with their start and end apart: 9, of which 5 were waited for; matrix products, arithmetic and copies ran while one was open for 11% of the time, Pallas kernels for 45%

profile of v1, /device:TPU:0, one launch (start us, length us, event | category | flops | bytes accessed | tf_op | source)
XLA Modules:
  0.0 1090.0 jit_solution(2245601383260790223)
XLA Ops:
  8.9 3.2 collective-permute-start
  12.1 34.4 %collective-permute-done = bf16[384,2048]{1,0:T(8,128)(2,1)S(1)} collective-permute-done((bf16[384,2048]{1,0:T(8,128)(2,1)S(1)}, bf16[384,2048]{1,0:T(8,128)(2,1)S(1)}, u32[]{:S(2)}, u32[]{:S(2)}) %collective-permute-start) | collective-permute-done | bytes 1572896 | tf_op jit(solution)/shard_map/ppermute | solution.py:517
  51.8 33.8 %collective-permute-done.1 = bf16[384,2048]{1,0:T(8,128)(2,1)S(1)} collective-permute-done((bf16[384,2048]{1,0:T(8,128)(2,1)S(1)}, bf16[384,2048]{1,0:T(8,128)(2,1)S(1)}, u32[]{:S(2)}, u32[]{:S(2)}) %collective-permute-start.1) | collective-permute-done | bytes 1572896 | tf_op jit(solution)/shard_map/ppermute | solution.py:517
  87.7 2.9 constant_dynamic-slice_fusion.1
  90.6 2.2 copy.43
  92.8 2.0 copy.42
  94.8 2.0 copy.45
  96.9 2.0 copy.44
  100.3 2.7 dynamic-slice_dynamic-update-slice_fusion.5
  102.9 2.0 dynamic-slice_dynamic-update-slice_fusion.4
  104.9 2.0 dynamic-slice_dynamic-update-slice_fusion.3
  116.3 2.9 fusion.13.kpre_ref
  119.2 13.9 %fusion.8 = (f32[6144,64]{1,0:T(8,128)}, f32[6144,64]{1,0:T(8,128)}, f32[6144,64]{1,0:T(8,128)}) fusion(f32[64]{0:T(128)S(1)} %multiply_power_fusion, f32[6144]{0:T(1024)S(1)} %iota_convert_fusion), kind=kLoop, calls=%fused_computation.34 | loop fusion | flops 786432 | bytes 4743424 | tf_op jit(solution)/shard_map/neg | solution.py:258
  133.2 9.5 pad_maximum_fusion.1
  142.7 17.3 %fusion.12.qa_ref.qb_ref = f32[768,4096]{1,0:T(8,128)} fusion(bf16[768,2048]{1,0:T(8,128)(2,1)} %bitcast.92, bf16[2048,4096]{1,0:T(8,128)(2,1)S(1)} %bitcast.70), kind=kOutput, calls=%fused_computation.59 | convolution fusion | flops 12884901888 | bytes 32505856 | tf_op jit(solution)/shard_map/dot_general | solution.py:20
  160.0 11.3 %all-gather.11.cloned.1.call-done.x_ref = bf16[16,384,2048]{2,1,0:T(8,128)(2,1)} async-done(((bf16[2,384,2048]{2,1,0:T(8,128)(2,1)}), bf16[16,384,2048]{2,1,0:T(8,128)(2,1)}) %all-gather.11.cloned.1.call-update) | async-done | bytes 25165840 | tf_op jit(solution)/shard_map/all_gather | solution.py:519
  171.3 41.2 %qkv.1 = (bf16[6144,2048]{1,0:T(8,128)(2,1)}, f32[6144,512]{1,0:T(8,128)}, f32[6144,128]{1,0:T(8,128)}, bf16[6144,512]{1,0:T(8,128)(2,1)}, bf16[6144,128]{1,0:T(...) custom-call(bf16[16,384,2048]{2,1,0:T(8,128)(2,1)} %all-gather.11.cloned.1.call-done.x_, ...), custom_call_target="tpu_custom_call" | custom-call | flops 19327352832 | bytes 100663296 | tf_op jit(solution)/shard_map/qkv/pallas_call | solution.py:313
  212.5 77.6 %shard_map.160 = (bf16[6144,256]{1,0:T(8,128)(2,1)}, f32[6144,256]{1,0:T(8,128)}) custom-call(bf16[6144,512]{1,0:T(8,128)(2,1)} %get-tuple-element.59.q_ref.refs_0_, bf16[128,6144]{1,0:T(8,128)(2,1)} %get-tuple-element.60.kt_ref.refs_1_.refs_4_, bf16[6144,128]{1,0:T(8,128)(2,1)} %get-tuple-element.61.v_ref.refs_2_), custom_call_target="tpu_custom_call" | custom-call | flops 19327352832 | bytes 25165824 | tf_op jit(solution)/shard_map/pallas_call | solution.py:97
  290.2 4.5 all-gather.13.cloned.1.call-done.g_ref
  294.7 37.9 %out_grad.2 = (bf16[6144,256]{1,0:T(8,128)(2,1)}, f32[256,2048]{1,0:T(8,128)}) custom-call(bf16[16,384,2048]{2,1,0:T(8,128)(2,1)} %all-gather.13.cloned.1.call-done.g_ref, bf16[2048,256]{1,0:T(8,128)(2,1)} %maximum_bitcast_fusion.w_ref, bf16[6144,256]{1,0:T(8,128)(2,1)} %get-tuple-element.62.o_ref.refs_2_), custom_call_target="tpu_custom_call" | custom-call | flops 12884901888 | bytes 25165824 | tf_op jit(solution)/shard_map/out_grad/pallas_call | solution.py:338
  332.6 2.3 dynamic-slice_bitcast_fusion.4.refs_4_
  334.9 80.9 %shard_map.161 = (bf16[6144,256]{1,0:T(8,128)(2,1)}, f32[6144,256]{1,0:T(8,128)}, bf16[16,384,256]{2,1,0:T(8,128)(2,1)}, f32[128,2048]{1,0:T(8,128)}) custom-call(bf16[6144,512]{1,0:T(8,128)(2,1)} %get-tuple-element.59.q_ref.refs_0_, bf16[128,6144]{1,0:T(8,128)(2,1)} %get-tuple-element.60.kt_ref.refs_1_.refs_4_, ...), custom_call_target="tpu_custom_call" | custom-call | flops 19327352832 | bytes 25165824 | tf_op jit(solution)/shard_map/pallas_call | solution.py:97
  415.9 2.4 bitcast_add_fusion.2
  418.3 38.4 %out_grad.3 = (bf16[6144,256]{1,0:T(8,128)(2,1)}, f32[256,2048]{1,0:T(8,128)}) custom-call(bf16[16,384,2048]{2,1,0:T(8,128)(2,1)} %all-gather.13.cloned.1.call-done.g_ref, bf16[2048,256]{1,0:T(8,128)(2,1)} %maximum_bitcast_fusion.1.w_ref, bf16[6144,256]{1,0:T(8,128)(2,1)} %get-tuple-element.71.o_ref.refs_2_), custom_call_target="tpu_custom_call" | custom-call | flops 12884901888 | bytes 25165824 | tf_op jit(solution)/shard_map/out_grad/pallas_call | solution.py:338
  456.7 2.3 dynamic-slice_bitcast_fusion.3.refs_8_
  459.0 108.8 %shard_map.162 = (bf16[6144,256]{1,0:T(8,128)(2,1)}, f32[128,6144]{1,0:T(8,128)}, f32[128,6144]{1,0:T(8,128)}, bf16[16,384,256]{2,1,0:T(8,128)(2,1)}, f32[128,2048]{1,0:T(8,128)}) custom-call(bf16[6144,512]{1,0:T(8,128)(2,1)} %get-tuple-element.59.q_ref.refs_0_, bf16[6144,256]{1,0:T(8,128)(2,1)} %get-tuple-element.65.refs_1_, ...), custom_call_target="tpu_custom_call" | custom-call | flops 48318382080 | bytes 50331648 | tf_op jit(solution)/shard_map/pallas_call | solution.py:97
  567.8 2.4 bitcast_add_fusion.1
  570.8 22.5 %shard_map.163 = f32[256,2048]{1,0:T(8,128)} custom-call(bf16[6144,256]{1,0:T(8,128)(2,1)} %get-tuple-element.76.refs_0_, f32[6144,512]{1,0:T(8,128)} %get-tuple-element.77.refs_1_, f32[1,128]{1,0:T(1,128)} %get-tuple-element.142.qn_ref.refs_2_, f32[6144,128]{1,0:T(8,128)} %get-tuple-element.139.cos_ref.refs_3_, ...), custom_call_target="tpu_custom_call" | custom-call | flops 6442450944 | bytes 37748736 | tf_op jit(solution)/shard_map/pallas_call | solution.py:97
  593.3 2.3 dynamic-slice_bitcast_fusion.2.refs_8_
  595.6 109.5 %shard_map.164 = (bf16[6144,256]{1,0:T(8,128)(2,1)}, f32[128,6144]{1,0:T(8,128)}, f32[128,6144]{1,0:T(8,128)}, bf16[16,384,256]{2,1,0:T(8,128)(2,1)}, f32[128,2048]{1,0:T(8,128)}) custom-call(bf16[6144,512]{1,0:T(8,128)(2,1)} %get-tuple-element.59.q_ref.refs_0_, bf16[6144,256]{1,0:T(8,128)(2,1)} %get-tuple-element.79.refs_1_, ...), custom_call_target="tpu_custom_call" | custom-call | flops 48318382080 | bytes 50331648 | tf_op jit(solution)/shard_map/pallas_call | solution.py:97
  705.2 2.8 bitcast_add_fusion
  708.1 4.7 broadcast_select_fusion
  713.1 5.4 collective-permute-done.2
  718.6 2.8 select_add_fusion.refs_6_
  721.4 72.8 %shard_map.165 = (f32[384,2048]{1,0:T(8,128)}, bf16[6144,128]{1,0:T(8,128)(2,1)}, bf16[16,384,256]{2,1,0:T(8,128)(2,1)}) custom-call(bf16[6144,256]{1,0:T(8,128)(2,1)} %get-tuple-element.83.refs_0_, f32[6144,512]{1,0:T(8,128)} %get-tuple-element.77.refs_1_, f32[1,128]{1,0:T(1,128)} %get-tuple-element.142.qn_ref.refs_2_, ...), custom_call_target="tpu_custom_call" | custom-call | flops 9663676416 | bytes 37748736 | tf_op jit(solution)/shard_map/pallas_call | solution.py:97
  798.7 97.9 %shard_map.166 = (bf16[2,384,2048]{2,1,0:T(8,128)(2,1)}, bf16[16,384,128]{2,1,0:T(8,128)(2,1)}, f32[192,2048]{1,0:T(8,128)}) custom-call(bf16[4,2,2,384,256]{4,3,2,1,0:T(8,128)(2,1)} %bitcast.101, bf16[4,2,2,384,256]{4,3,2,1,0:T(8,128)(2,1)} %bitcast.102, bf16[4096,2048]{1,0:T(8,128)(2,1)} %refs_3_.1, bf16[4096,2048]{1,0:T(8,128)(2,1)} %refs_3_.1, ...), custom_call_target="tpu_custom_call" | custom-call | flops 12884901888 | bytes 30000000 | tf_op jit(solution)/shard_map/pallas_call | solution.py:97
  896.6 2.8 fusion.5
  901.1 54.5 %hidden_grad.1 = (bf16[2,384,2048]{2,1,0:T(8,128)(2,1)}, f32[8,128]{1,0:T(8,128)}, f32[8,128]{1,0:T(8,128)}, f32[8,2048]{1,0:T(8,128)}) custom-call(bf16[4,2,2,384,256]{4,3,2,1,0:T(8,128)(2,1)} %bitcast.88, bf16[4,2,2,384,256]{4,3,2,1,0:T(8,128)(2,1)} %bitcast.89, bf16[4,2,2,384,128]{4,3,2,1,0:T(8,128)(2,1)} %bitcast.97, f32[768,4096]{1,0:T(8,128)} %fusion.12.qa_ref.qb_ref, ...), custom_call_target="tpu_custom_call" | custom-call | flops 16106127360 | bytes 50000000 | tf_op jit(solution)/shard_map/hidden_grad/pallas_call | solution.py:472
  957.8 33.4 %psum.7 = f32[2304]{0:T(1024)S(1)} all-reduce(f32[2304]{0:T(1024)S(1)} %pad_maximum_fusion.5), channel_id=1, replica_groups=mesh['cp'=16] {'cp'}, use_global_device_ids=true, to_apply=%region_4.5 | all-reduce | flops 2304 | bytes 18432 | tf_op jit(solution)/shard_map/psum | solution.py:583
  992.3 12.5 %pad_maximum_fusion = f32[16,2,128,2048]{3,2,0,1:T(8,128)S(1)} fusion(f32[16,1,128,2048]{3,2,0,1:T(8,128)} %bitcast.81, f32[16,1,128,2048]{3,2,0,1:T(8,128)} %bitcast.82), kind=kLoop, calls=%fused_computation | loop fusion | flops 8388608 | bytes 67108864 | tf_op jit(solution)/shard_map/stack | solution.py:560
  1004.9 11.3 %copy.39 = f32[16,2,128,2048]{3,2,1,0:T(8,128)} copy(f32[16,2,128,2048]{3,2,0,1:T(8,128)S(1)} %pad_maximum_fusion) | data formatting | bytes 67108864 | tf_op jit(solution)/shard_map/stack | solution.py:560
  1016.1 19.1 %place.2.refs_1_ = f32[2048,4096]{1,0:T(8,128)} custom-call(f32[16,128,2048]{2,1,0:T(8,128)} %bitcast.78), custom_call_target="tpu_custom_call" | custom-call | flops 1000000 | bytes 35000000 | tf_op jit(solution)/shard_map/place/pallas_call | solution.py:490
  1035.3 7.8 slice.34
  1043.0 19.2 %place.3 = f32[2048,4096]{1,0:T(8,128)} custom-call(f32[16,192,2048]{2,1,0:T(8,128)} %bitcast.72, f32[2048,4096]{1,0:T(8,128)} %place.2.refs_1_), custom_call_target="tpu_custom_call", output_to_operand_aliasing={{}: (1, {})} | custom-call | flops 1000000 | bytes 35000000 | tf_op jit(solution)/shard_map/place/pallas_call | solution.py:490
  1062.2 4.0 copy.47
  1066.2 4.0 fusion.10
  1070.1 5.3 copy.40
  1075.5 5.5 copy.41
  (106 shorter events, 31.7 us)
Async XLA Ops:
  7.2 164.1 %all-gather.11.cloned.1.call-start = ((), (), s32[]{:S(2)}) async-start(), calls=%async_computation | async-start | bytes 28311552 | tf_op jit(solution)/shard_map/all_gather | solution.py:519
  8.8 37.6 %copy-start.2 = (bf16[2,384,2048]{2,1,0:T(8,128)(2,1)S(1)}, bf16[2,384,2048]{2,1,0:T(8,128)(2,1)}, u32[]{:S(2)}) copy-start(bf16[2,384,2048]{2,1,0:T(8,128)(2,1)} %x_ref.1) | copy-start | bytes 9437188
  8.9 37.6 %collective-permute-start = (bf16[384,2048]{1,0:T(8,128)(2,1)S(1)}, bf16[384,2048]{1,0:T(8,128)(2,1)S(1)}, u32[]{:S(2)}, u32[]{:S(2)}) collective-permute-start(bf16[384,2048]{1,0:T(8,128)(2,1)S(1)} %dynamic-slice_bitcast_fusion.1), channel_id=1, source_target_pairs={{0,2},{1,3},{2,0},{3,1},{4,6},{5,7},{6,4},{7,5},{8,10},{9,11},{10,... | collective-permute-start | bytes 4718600 | tf_op jit(solution)/shard_map/ppermute | solution.py:517
  46.7 1.7 copy-start.1
  48.4 246.3 %all-gather.13.cloned.1.call-start = ((), (), s32[]{:S(2)}) async-start(), calls=%async_computation.1 | async-start | bytes 28311552 | tf_op jit(solution)/shard_map/all_gather | solution.py:519
  50.0 35.6 %copy-start.4 = (bf16[2,384,2048]{2,1,0:T(8,128)(2,1)S(1)}, bf16[2,384,2048]{2,1,0:T(8,128)(2,1)}, u32[]{:S(2)}) copy-start(bf16[2,384,2048]{2,1,0:T(8,128)(2,1)} %g_ref.1) | copy-start | bytes 9437188
  50.0 35.6 %collective-permute-start.1 = (bf16[384,2048]{1,0:T(8,128)(2,1)S(1)}, bf16[384,2048]{1,0:T(8,128)(2,1)S(1)}, u32[]{:S(2)}, u32[]{:S(2)}) collective-permute-start(bf16[384,2048]{1,0:T(8,128)(2,1)S(1)} %dynamic-slice_bitcast_fusion), channel_id=1, source_target_pairs={{0,2},{1,3},{2,0},{3,1},{4,6},{5,7},{6,4},{7,5},{8,10},{9,11},{10,... | collective-permute-start | bytes 4718600 | tf_op jit(solution)/shard_map/ppermute | solution.py:517
  51.8 35.9 %copy-start.20 = (bf16[2048]{0:T(1024)(128)(2,1)S(1)}, bf16[2048]{0:T(1024)(128)(2,1)}, u32[]{:S(2)}) copy-start(bf16[2048]{0:T(1024)(128)(2,1)} %param.15) | copy-start | bytes 12292
  85.8 1.7 copy-start.3
  87.6 904.8 %all-gather.21.cloned.1.call-start = ((), (), s32[]{:S(2)}) async-start(), calls=%async_computation.5 | async-start | bytes 17825792 | tf_op jit(solution)/shard_map/all_gather | solution.py:513
  87.7 26.1 %copy-start.19 = (f32[2048]{0:T(1024)}, f32[2048]{0:T(1024)S(1)}, u32[]{:S(2)}) copy-start(f32[2048]{0:T(1024)S(1)} %convert_element_type.32) | copy-start | bytes 24580
  90.6 8.3 copy-start.23
  90.6 8.4 copy-start.24
  90.6 8.9 copy-start
  98.9 20.3 %copy-start.21 = (f32[64]{0:T(128)}, f32[64]{0:T(128)S(1)}, u32[]{:S(2)}) copy-start(f32[64]{0:T(128)S(1)} %multiply_power_fusion) | copy-start | bytes 772
  99.5 9.2 copy-start.10
  100.2 11.3 %copy-start.15 = (bf16[128,2048]{0,1:T(8,128)(2,1)S(1)}, bf16[128,2048]{0,1:T(8,128)(2,1)}, u32[]{:S(2)}) copy-start(bf16[128,2048]{0,1:T(8,128)(2,1)} %copy.43) | copy-start | bytes 1572868
  100.2 11.3 %copy-start.16 = (bf16[128,2048]{0,1:T(8,128)(2,1)S(1)}, bf16[128,2048]{0,1:T(8,128)(2,1)}, u32[]{:S(2)}) copy-start(bf16[128,2048]{0,1:T(8,128)(2,1)} %copy.42) | copy-start | bytes 1572868
  104.9 7.7 copy-start.17
  104.9 7.7 copy-start.18
  114.6 1.7 copy-start.12
  116.3 26.4 %slice-start = ((s8[16777216]{0:T(1024)(128)(4,1)}), s8[4194304]{0:T(1024)(128)(4,1)S(1)}, s32[]{:S(2)}) async-start(s8[16777216]{0:T(1024)(128)(4,1)} %bitcast.69), calls=%async_computation.6 | async-start | bytes 8388608
  116.3 26.4 %slice-start.1 = ((s8[16777216]{0:T(1024)(128)(4,1)}), s8[4194304]{0:T(1024)(128)(4,1)S(1)}, s32[]{:S(2)}) async-start(s8[16777216]{0:T(1024)(128)(4,1)} %bitcast.69), calls=%async_computation.7 | async-start | bytes 8388608
  119.2 23.4 %slice-start.2 = ((s8[16777216]{0:T(1024)(128)(4,1)}), s8[4194304]{0:T(1024)(128)(4,1)S(1)}, s32[]{:S(2)}) async-start(s8[16777216]{0:T(1024)(128)(4,1)} %bitcast.69), calls=%async_computation.8 | async-start | bytes 8388608
  133.2 9.5 slice-start.3
  334.9 80.9 %copy-start.14 = (f32[256,2048]{1,0:T(8,128)S(1)}, f32[256,2048]{1,0:T(8,128)}, u32[]{:S(2)}) copy-start(f32[256,2048]{1,0:T(8,128)} %get-tuple-element.63) | copy-start | bytes 6291460
  459.0 108.8 %copy-start.13 = (f32[256,2048]{1,0:T(8,128)S(1)}, f32[256,2048]{1,0:T(8,128)}, u32[]{:S(2)}) copy-start(f32[256,2048]{1,0:T(8,128)} %get-tuple-element.72) | copy-start | bytes 6291460
  570.2 422.2 %all-gather.19.cloned.1.call-start = ((), (), s32[]{:S(2)}) async-start(), calls=%async_computation.4 | async-start | bytes 17825792 | tf_op jit(solution)/shard_map/all_gather | solution.py:513
  570.8 445.4 %all-gather.17.cloned.1.call-start = ((), (), s32[]{:S(2)}) async-start(), calls=%async_computation.3 | async-start | bytes 17825792 | tf_op jit(solution)/shard_map/all_gather | solution.py:513
  595.6 109.6 %copy-start.9 = (f32[256,2048]{1,0:T(8,128)S(1)}, f32[256,2048]{1,0:T(8,128)}, u32[]{:S(2)}) copy-start(f32[256,2048]{1,0:T(8,128)} %shard_map.163) | copy-start | bytes 6291460
  705.2 2.9 copy-start.5
  708.0 327.2 %all-gather.15.cloned.1.call-start = ((), (), s32[]{:S(2)}) async-start(), calls=%async_computation.2 | async-start | bytes 26738688 | tf_op jit(solution)/shard_map/all_gather | solution.py:513
  708.1 10.4 copy-start.6
  708.1 10.4 copy-start.7
  708.1 10.4 copy-start.8
  712.9 5.7 collective-permute-start.2
  896.6 2.8 copy-start.22
  1075.5 5.5 copy-start.11
Sparse Core Ops, SparseCore 0:
  48.5 122.7 all-gather.10
  173.2 121.4 all-gather.12
  570.3 112.3 all-gather.20
  684.8 105.9 all-gather.18
  793.5 118.8 all-gather.16
  915.0 104.2 all-gather.14

commit v2 on v1

v2 whole, which is shorter than its diff:
```python
import functools
import math

import jax
import jax.numpy as jnp
from jax import lax
from jax.experimental import pallas as pl
from jax.experimental.pallas import tpu as pltpu
from jax.sharding import PartitionSpec as P


ROPE_THETA = 1000000.0
NORM_EPS = 1e-6
HEAD_DIM=128; F32=jnp.float32; BF16=jnp.bfloat16
SCALE = HEAD_DIM ** -0.5
EXP2_SCALE = SCALE * math.log2(math.e)
UR = 256
TILING = (2, 2, 1024)


def nn(a, b): return lax.dot_general(a, b, (((1,), (0,)), ((), ())), preferred_element_type=F32)


def nt(a, b): return lax.dot_general(a, b, (((1,), (1,)), ((), ())), preferred_element_type=F32)


def lanes(i): return slice(i * HEAD_DIM, (i + 1) * HEAD_DIM)


def params(**more):
    return pltpu.CompilerParams(dimension_semantics=("arbitrary",), vmem_limit_bytes=60000000, **more)


def cost(flops, nbytes):
    return pl.CostEstimate(flops=flops, bytes_accessed=nbytes, transcendentals=0)


def fixed(*shape):
    return pl.BlockSpec(shape, lambda t: (0,) * len(shape))


def whole(a):
    return fixed(*a.shape)


def row_spec(rows, width, shift=0, col=0):
    return pl.BlockSpec((rows, width), lambda t: (t + shift, col))


def grid_step():
    return pl.program_id(0)


def row_of(reduce, x):
    return reduce(x, axis=-1, keepdims=True)


def row_mean(x):
    return row_of(jnp.mean, x)


def row_scale(x):
    return lax.rsqrt(row_mean(x * x) + NORM_EPS)


SPLIT = 12
OTHERS = tuple(range(1, 16))
FLIPS = {"all": OTHERS, "low": OTHERS, "high": OTHERS, "half": (2,), "other": (1,)}


def carrying(kernel, n_in, n_out, n_scratch, steps, kinds):
    if not kinds:
        return kernel
    m = sum(2 if kind == "other" else 1 for kind in kinds)

    def body(*refs):
        ins, srcs, refs = refs[:n_in], refs[n_in:n_in + m], refs[n_in + m:]
        outs, dsts, refs = refs[:n_out], refs[n_out:n_out + len(kinds)], refs[n_out + len(kinds):]
        scratch, sems = refs[:n_scratch], refs[n_scratch:]
        step = grid_step()
        me = lax.axis_index('cp')

        def remote(src, dst, send, recv, peer):
            return pltpu.make_async_remote_copy(src_ref=src, dst_ref=dst, send_sem=send, recv_sem=recv, device_id=(peer,), device_id_type=pl.DeviceIdType.MESH)

        def each(send_part, recv_part, local_part):
            def act(copy):
                send_part(copy)
                recv_part(copy)

            first = 0
            for i, kind in enumerate(kinds):
                send, recv, own = sems[3 * i:3 * i + 3]
                src, dst = srcs[first], dsts[i]
                if kind == "all":
                    for n, flip in enumerate(FLIPS[kind]):
                        act(remote(src.at[me ^ flip], dst.at[me], send.at[n], recv.at[n], me ^ flip))
                    local_part(pltpu.make_async_copy(src.at[me], dst.at[me], own))
                elif kind in ("low", "high"):
                    base = 0 if kind == "low" else SPLIT
                    chosen = (lambda dev: dev < SPLIT) if kind == "low" else (lambda dev: dev >= SPLIT)
                    for n, flip in enumerate(FLIPS[kind]):
                        peer = me ^ flip

                        @pl.when(chosen(peer))
                        def _():
                            send_part(remote(src.at[peer - base], dst.at[me], send.at[n], recv.at[n], peer))

                        @pl.when(chosen(me))
                        def _():
                            recv_part(remote(src.at[0], dst.at[peer], send.at[n], recv.at[n], peer))

                    @pl.when(chosen(me))
                    def _():
                        local_part(pltpu.make_async_copy(src.at[me - base], dst.at[me], own))
                elif kind == "half":
                    rows = dst.shape[0]
                    theirs = pl.multiple_of((1 - (me // 2) % 2) * rows, rows)
                    act(remote(src.at[pl.ds(theirs, rows)], dst, send.at[0], recv.at[0], me ^ 2))
                else:
                    @pl.when(me % 2 == 0)
                    def _():
                        act(remote(srcs[first + 1], dst, send.at[0], recv.at[0], me ^ 1))

                    @pl.when(me % 2 == 1)
                    def _():
                        act(remote(src, dst, send.at[0], recv.at[0], me ^ 1))

                    first += 1
                first += 1

        @pl.when(step == 0)
        def _():
            meet(me, sorted({flip for kind in kinds for flip in FLIPS[kind]}))
            each(lambda copy: copy.start(), lambda copy: None, lambda copy: copy.start())

        kernel(*ins, *outs, *scratch)

        @pl.when(step == steps - 1)
        def _():
            each(lambda copy: copy.wait_send(), lambda copy: copy.wait_recv(), lambda copy: copy.wait())

    return body


def meet(me, flips):
    barrier = pltpu.get_barrier_semaphore()
    for flip in flips:
        pl.semaphore_signal(barrier, inc=1, device_id=(me ^ flip,), device_id_type=pl.DeviceIdType.MESH)
    pl.semaphore_wait(barrier, len(flips))


def call(kernel, grid, in_specs, out_specs, out_shape, scratch, estimate, operands, carry=(), key=None, aliases=None):
    kinds = [kind for kind, *_ in carry]
    sources = [a for _, *arrays in carry for a in arrays]
    hbm = pl.BlockSpec(memory_space=pltpu.HBM)
    sems, received = [], []
    for kind, a, *_ in carry:
        count = len(FLIPS[kind])
        sems += [pltpu.SemaphoreType.DMA((count,)), pltpu.SemaphoreType.DMA((count,)), pltpu.SemaphoreType.DMA]
        count = a.shape[0] // 2 if kind == "half" else 16 if kind in ("low", "high") else a.shape[0]
        received.append(jax.ShapeDtypeStruct((count,) + a.shape[1:], a.dtype))
    more = dict(collective_id=key, has_side_effects=True) if kinds else {}
    return pl.pallas_call(
        carrying(kernel, len(operands), len(out_shape), len(scratch), grid, kinds), grid=(grid,),
        in_specs=list(in_specs) + [hbm] * len(sources), out_specs=list(out_specs) + [hbm] * len(kinds),
        out_shape=list(out_shape) + received, scratch_shapes=list(scratch) + sems, compiler_params=params(**more), cost_estimate=estimate,
        input_output_aliases=aliases or {},
    )(*operands, *sources)


def key_mask(width):
    return lax.broadcasted_iota(jnp.int32, (UR, width), 0) + (width - UR) >= lax.broadcasted_iota(jnp.int32, (UR, width), 1)


def flash_fwd_kernel(nh, rh, tk, begin, q_ref, kt_ref, v_ref, *refs):
    o_ref, lse_ref, s_ref, acc_ref, m_ref, l_ref = refs[-6:]
    tile = grid_step() + begin
    tq = rh * UR
    classes = tk // tq
    units = [(r, head) for r in range(rh) for head in range(nh)]
    m_ref[:] = jnp.full_like(m_ref, -jnp.inf)
    l_ref[:] = jnp.zeros_like(l_ref)
    acc_ref[:] = jnp.zeros_like(acc_ref)
    query = lambda u: q_ref[u[0] * UR:(u[0] + 1) * UR, lanes(u[1])]
    for n, u in enumerate(units):
        s_ref[n] = nn(query(u), kt_ref[:, :tk])

    def update(n, keys, scores, width):
        top = scores[:, :HEAD_DIM]
        for piece in range(1, width // HEAD_DIM):
            top = jnp.maximum(top, scores[:, lanes(piece)])
        m_prev = m_ref[n]
        m_new = jnp.maximum(m_prev, row_of(jnp.max, top))
        alpha = jnp.exp2((m_prev - m_new) * EXP2_SCALE)
        shift = m_new * EXP2_SCALE
        part, pieces = None, []
        for piece in range(width // HEAD_DIM):
            prob = jnp.exp2(scores[:, lanes(piece)] * EXP2_SCALE - shift)
            part = prob if part is None else part + prob
            pieces.append(prob.astype(BF16))
        m_ref[n] = m_new
        l_ref[n] = l_ref[n] * alpha + part
        acc_ref[n] = acc_ref[n] * alpha + nn(jnp.hstack(pieces), v_ref[keys, :])

    last = tile // classes

    @pl.loop(0, last)
    def _(j):
        keys = pl.ds(pl.multiple_of(j * tk, tk), tk)
        following = pl.ds(pl.multiple_of(j * tk + tk, tk), tk)
        for n, u in enumerate(units):
            update(n, keys, s_ref[n], tk)
            s_ref[n] = nn(query(u), kt_ref[:, following])

    for c in range(classes):
        @pl.when(tile % classes == c)
        def _():
            for n, u in enumerate(units):
                width = c * tq + (u[0] + 1) * UR
                keys = pl.ds(pl.multiple_of(last * tk, tk), width)
                update(n, keys, jnp.where(key_mask(width), s_ref[n, :, :width], -jnp.inf), width)

    for n, u in enumerate(units):
        rows = slice(u[0] * UR, (u[0] + 1) * UR)
        total = row_of(jnp.sum, l_ref[n])
        o_ref[rows, lanes(u[1])] = (acc_ref[n] / total).astype(BF16)
        lse_ref[rows, lanes(u[1])] = m_ref[n] * EXP2_SCALE + jnp.log2(total)


def run_fwd(q, kt, v, chunk, carry=(), key=None, tiles=None, into=()):
    nh, rh, tk = TILING
    seq, width, tq = q.shape[0], nh * HEAD_DIM, rh * UR
    begin, end = tiles or (0, seq // tq)
    out = row_spec(tq, width, begin)
    stat = pltpu.VMEM((nh * rh, UR, HEAD_DIM), F32)
    sds = jax.ShapeDtypeStruct
    share = (end * end - begin * begin) * tq * tq / (seq * seq)
    return call(functools.partial(flash_fwd_kernel, nh, rh, tk, begin), end - begin,
                [row_spec(tq, width, begin, chunk), whole(kt), whole(v)] + [pl.BlockSpec(memory_space=pltpu.HBM)] * len(into), [out, out],
                [sds((seq, width), BF16), sds((seq, width), F32)], [pltpu.VMEM((nh * rh, UR, tk), F32), stat, stat, stat],
                cost(int(2 * seq * seq * width * share), seq * 4096), (q, kt, v, *into), carry, key, {3: 0, 4: 1} if into else None)


def flash_bwd_kernel(nh, rh, tk, begin, end, first, q_ref, do_ref, o_ref, lse_ref, kt_ref, vt_ref, k_ref, *refs):
    dk0_ref, dv0_ref = (None, None) if first else refs[:2]
    dq_ref, dkt_ref, dvt_ref, acc_ref, qt_ref, dot_ref, delta_ref, p_ref, ds_ref = refs[-9:]
    tile = grid_step() + begin
    tq = rh * UR
    classes = tk // tq
    units = [(r, head) for r in range(rh) for head in range(nh)]
    rows_of = lambda u: slice(u[0] * UR, (u[0] + 1) * UR)
    at = lambda n: slice(n * UR, (n + 1) * UR)

    @pl.when(tile == begin)
    def _():
        dkt_ref[:] = jnp.zeros_like(dkt_ref) if first else dk0_ref[:]
        dvt_ref[:] = jnp.zeros_like(dvt_ref) if first else dv0_ref[:]

    acc_ref[:] = jnp.zeros_like(acc_ref)
    for n, u in enumerate(units):
        qt_ref[:, at(n)] = q_ref[rows_of(u), lanes(u[1])].astype(F32).T.astype(BF16)
        do = do_ref[rows_of(u), lanes(u[1])].astype(F32)
        dot_ref[:, at(n)] = do.T.astype(BF16)
        delta = row_of(jnp.sum, do * o_ref[rows_of(u), lanes(u[1])].astype(F32))
        delta_ref[n] = jnp.broadcast_to(delta, (UR, HEAD_DIM))

    def unit(n, u, keys, width, masked):
        scores = nn(q_ref[rows_of(u), lanes(u[1])], kt_ref[:, keys])
        if masked:
            scores = jnp.where(key_mask(width), scores, -jnp.inf)
        d_prob = nn(do_ref[rows_of(u), lanes(u[1])], vt_ref[:, keys])
        lse, delta = lse_ref[rows_of(u), lanes(u[1])], delta_ref[n]
        for piece in range(width // HEAD_DIM):
            prob = jnp.exp2(scores[:, lanes(piece)] * EXP2_SCALE - lse)
            p_ref[at(n), lanes(piece)] = prob.astype(BF16)
            ds_ref[at(n), lanes(piece)] = (prob * (d_prob[:, lanes(piece)] - delta)).astype(BF16)

    def products(rows, keys, width):
        dvt_ref[:, keys] += nn(dot_ref[:, rows], p_ref[rows, :width])
        dkt_ref[:, keys] += nn(qt_ref[:, rows], ds_ref[rows, :width])
        acc_ref[rows, :] += nn(ds_ref[rows, :width], k_ref[keys, :])

    last = tile // classes

    @pl.loop(0, last)
    def _(j):
        keys = pl.ds(pl.multiple_of(j * tk, tk), tk)
        for n, u in enumerate(units):
            unit(n, u, keys, tk, False)
        products(slice(0, len(units) * UR), keys, tk)

    for c in range(classes):
        @pl.when(tile % classes == c)
        def _():
            for r in range(rh):
                width = c * tq + (r + 1) * UR
                keys = pl.ds(pl.multiple_of(last * tk, tk), width)
                for n, u in enumerate(units):
                    if u[0] == r:
                        unit(n, u, keys, width, True)
                products(slice(r * nh * UR, (r + 1) * nh * UR), keys, width)

    for n, u in enumerate(units):
        dq_ref[rows_of(u), lanes(u[1])] = (acc_ref[at(n), :] * SCALE).astype(BF16)

    if end < 0:
        @pl.when(tile == begin + pl.num_programs(0) - 1)
        def _():
            dkt_ref[:] = dkt_ref[:] * SCALE


def run_bwd(q, do, o, lse, kt, vt, k, chunk, carry=(), key=None, so_far=(), tiles=None, last=False, into=None):
    nh, rh, tk = TILING
    seq, width, tq, rows = q.shape[0], nh * HEAD_DIM, rh * UR, nh * rh * UR
    begin, end = tiles or (0, seq // tq)
    row = row_spec(tq, width, begin)
    sds = jax.ShapeDtypeStruct
    share = (end * end - begin * begin) * tq * tq / (seq * seq)
    held, start, height = [], 0, (end - begin) * tq
    if into is not None:
        held, start, height = [] if isinstance(into, str) else [into], begin, seq
    return call(functools.partial(flash_bwd_kernel, nh, rh, tk, begin, -1 if last else 0, not so_far), end - begin,
                [row_spec(tq, width, begin, chunk), row, row, row, whole(kt), whole(vt), whole(k)] + [whole(a) for a in so_far] + [pl.BlockSpec(memory_space=pltpu.HBM)] * len(held),
                [row_spec(tq, width, start), whole(kt), whole(kt)], [sds((height, width), BF16), sds(kt.shape, F32), sds(kt.shape, F32)],
                [pltpu.VMEM((rows, HEAD_DIM), F32), pltpu.VMEM((HEAD_DIM, rows), BF16), pltpu.VMEM((HEAD_DIM, rows), BF16),
                 pltpu.VMEM((nh * rh, UR, HEAD_DIM), F32), pltpu.VMEM((rows, tk), BF16), pltpu.VMEM((rows, tk), BF16)],
                cost(int(5 * seq * seq * width * share), seq * 8192), (q, do, o, lse, kt, vt, k, *so_far, *held), carry, key, {7 + len(so_far): 0} if held else None)


def tn(a, b):
    return nn(a.astype(F32).T.astype(BF16), b)


def inverse_frequencies():
    inv_freq = ROPE_THETA ** (-jnp.arange(0, HEAD_DIM, 2, dtype=F32) / HEAD_DIM)
    return jnp.concatenate([inv_freq, inv_freq]).reshape(1, HEAD_DIM)


def half_roll(x):
    return pltpu.roll(x, HEAD_DIM // 2, 1)


def head_finish(pre, gain, cos_t, sin_t):
    scale = row_scale(pre)
    normed = pre * scale * gain
    return normed * cos_t + half_roll(normed) * sin_t


def head_finish_bwd(pre, gain, cos_t, sin_t, d_rot):
    d_normed = d_rot * cos_t - half_roll(d_rot) * sin_t
    scale = row_scale(pre)
    unit = pre * scale
    d_unit = d_normed * gain
    return scale * (d_unit - unit * row_mean(d_unit * unit)), d_normed * unit


def slot_of(tok):
    return ((tok // 4) * 2 + tok % 2) * 2 + (tok // 2) % 2


PATHS = "t2m4m8m124282184684181" + "61a1c1e1"
HOPS = tuple(zip(PATHS[::2], (int(flip) for flip in PATHS[1::2])))


def place_of(source):
    return 0 if source in "tm" else int(source, 16)


def gather_kernel(steps, x_ref, gain_ref, wq_ref, wk_ref, wv_ref, freq_ref, local_ref, other_ref, qpre_ref, kpre_ref, cos_ref, sin_ref, w_ref, all_ref, swap_ref, h_ref, send, recv, own, swap_send, swap_recv):
    step = grid_step()
    me = lax.axis_index('cp')
    which = (me // 2) % 2
    mesh_id = pl.DeviceIdType.MESH

    def hop(n):
        source, flip = HOPS[n]
        block = me ^ place_of(source)
        src = local_ref.at[which] if source == "m" else local_ref.at[1 - which] if source == "t" else all_ref.at[block]
        return pltpu.make_async_remote_copy(src_ref=src, dst_ref=all_ref.at[block], send_sem=send.at[n], recv_sem=recv.at[n], device_id=(me ^ flip,), device_id_type=mesh_id)

    mine = pltpu.make_async_copy(local_ref.at[which], all_ref.at[me], own)
    swap = pltpu.make_async_remote_copy(src_ref=other_ref.at[1 - which], dst_ref=swap_ref, send_sem=swap_send, recv_sem=swap_recv, device_id=(me ^ 2,), device_id_type=mesh_id)

    @pl.when(step == 0)
    def _():
        meet(me, sorted({flip for _, flip in HOPS}))
        for n, (source, _) in enumerate(HOPS):
            if source in "tm":
                hop(n).start()
        mine.start()
        rows = x_ref.shape[1]
        for b in range(2):
            for first in range(0, rows, 128):
                x = x_ref[b, first:first + 128].astype(F32)
                scale = row_scale(x)
                h_ref[b * rows + first:b * rows + first + 128] = (x * scale * gain_ref[:]).astype(BF16)

    @pl.when(step < steps - 1)
    def _():
        qpre_ref[:] = nn(h_ref[:], wq_ref[:])
        span = cos_ref.shape[0]
        position = (step * span + lax.broadcasted_iota(jnp.int32, (span, HEAD_DIM), 0)).astype(F32)
        angles = position * freq_ref[:]
        cos_ref[:] = jnp.cos(angles)
        lower = lax.broadcasted_iota(jnp.int32, (span, HEAD_DIM), 1) < HEAD_DIM // 2
        sine = jnp.sin(angles)
        sin_ref[:] = jnp.where(lower, -sine, sine)

    group, half = me // 4, me % 2
    for j in range(2):
        for core in range(2):
            @pl.when((step == 2 * group + j) & (half == core))
            def _():
                for c in range(2):
                    w_ref[:, lanes(2 * c + j)] = wq_ref[:, lanes(2 * core + c)]
    for n in range(4):
        @pl.when((step == 0) & (group == n))
        def _():
            w_ref[:, lanes(4)] = wk_ref[:, lanes(n)]
            w_ref[:, lanes(5)] = wv_ref[:, lanes(n)]

    @pl.when(step == steps - 1)
    def _():
        kpre_ref[:] = nn(h_ref[:], wk_ref[:])
        for n, (source, flip) in enumerate(HOPS):
            if flip > 1:
                hop(n).wait_recv()
                for then, (needs, _) in enumerate(HOPS):
                    if needs not in "tm" and place_of(needs) == place_of(source) ^ flip:
                        hop(then).start()
                if source == "t":
                    swap.start()
        for n, (_, flip) in enumerate(HOPS):
            if flip == 1:
                hop(n).wait_recv()
        for n in range(len(HOPS)):
            hop(n).wait_send()
        mine.wait()
        swap.wait()


def run_gather(hidden_in, grad_out, gain, w_query, w_key, w_value, freq, seq, key):
    batch, rows, dim = hidden_in.shape
    width = w_key.shape[1]
    steps = w_query.shape[1] // width + 1
    tile = lambda t: (0, jnp.minimum(t, steps - 2))
    hbm = pl.BlockSpec(memory_space=pltpu.HBM)
    sds = jax.ShapeDtypeStruct
    one, count = pltpu.SemaphoreType.DMA, pltpu.SemaphoreType.DMA((len(HOPS),))
    both = batch * rows
    table = pl.BlockSpec((seq // (steps - 1), HEAD_DIM), lambda t: (jnp.minimum(t, steps - 2), 0))
    return pl.pallas_call(
        functools.partial(gather_kernel, steps), grid=(steps,), name="gather",
        in_specs=[whole(hidden_in), whole(gain), pl.BlockSpec((dim, width), tile), whole(w_key), whole(w_value), whole(freq), hbm, hbm],
        out_specs=[pl.BlockSpec((both, width), tile), fixed(both, width), table, table, fixed(dim, 6 * HEAD_DIM), hbm, hbm],
        out_shape=[sds((both, w_query.shape[1]), F32), sds((both, width), F32), sds((seq, HEAD_DIM), F32), sds((seq, HEAD_DIM), F32), sds((dim, 6 * HEAD_DIM), BF16), sds((16, rows, dim), BF16), sds((rows, dim), BF16)],
        scratch_shapes=[pltpu.VMEM((both, dim), BF16), count, count, one, one, one],
        compiler_params=params(collective_id=key, has_side_effects=True), cost_estimate=cost(2 * both * dim * 4608, 60000000),
    )(hidden_in, gain, w_query, w_key, w_value, freq, hidden_in, grad_out)


def qkv_kernel(x_ref, gain_ref, w_ref, qn_ref, kn_ref, cos_ref, sin_ref, h_ref, qpre_ref, kpre_ref, q_ref, k_ref, kt_ref, v_ref, vt_ref):
    for first in range(0, x_ref.shape[0], 128):
        rs = slice(first, first + 128)
        x = x_ref[rs].astype(F32)
        scale = row_scale(x)
        h = (x * scale * gain_ref[:]).astype(BF16)
        h_ref[rs] = h
        pre = nn(h, w_ref[:])
        cos_t, sin_t = cos_ref[rs], sin_ref[rs]
        qpre_ref[rs] = pre[:, :4 * HEAD_DIM]
        for head in range(4):
            q_ref[rs, lanes(head)] = head_finish(pre[:, lanes(head)], qn_ref[:], cos_t, sin_t).astype(BF16)
        kpre = pre[:, lanes(4)]
        kpre_ref[rs] = kpre
        k_rot = head_finish(kpre, kn_ref[:], cos_t, sin_t)
        k_ref[rs] = k_rot.astype(BF16)
        kt_ref[:, rs] = k_rot.T.astype(BF16)
        v = pre[:, lanes(5)]
        v_ref[rs] = v.astype(BF16)
        vt_ref[:, rs] = v.T.astype(BF16)


def run_qkv(x, gain, w_all, qn, kn, cos_t, sin_t):
    seq, dim = x.shape
    rows = 512
    row = lambda width: row_spec(rows, width)
    col = pl.BlockSpec((HEAD_DIM, rows), lambda t: (0, t))
    sds = jax.ShapeDtypeStruct
    return pl.pallas_call(
        qkv_kernel, grid=(seq // rows,), name="qkv",
        in_specs=[row(dim), whole(gain), whole(w_all), whole(qn), whole(kn), row(HEAD_DIM), row(HEAD_DIM)],
        out_specs=[row(dim), row(4 * HEAD_DIM), row(HEAD_DIM), row(4 * HEAD_DIM), row(HEAD_DIM), col, row(HEAD_DIM), col],
        out_shape=[sds((seq, dim), BF16), sds((seq, 4 * HEAD_DIM), F32), sds((seq, HEAD_DIM), F32), sds((seq, 4 * HEAD_DIM), BF16),
                   sds((seq, HEAD_DIM), BF16), sds((HEAD_DIM, seq), BF16), sds((seq, HEAD_DIM), BF16), sds((HEAD_DIM, seq), BF16)],
        compiler_params=params(), cost_estimate=cost(2 * seq * dim * 768, seq * dim * 8),
    )(x, gain, w_all, qn, kn, cos_t, sin_t)


def out_grad_kernel(g_ref, w_ref, o_ref, do_ref, wg_ref):
    @pl.when(grid_step() == 0)
    def _():
        wg_ref[:] = jnp.zeros_like(wg_ref)

    g = g_ref[0]
    do_ref[:] = nn(g, w_ref[:]).astype(BF16)
    wg_ref[:] += tn(o_ref[:], g)


def run_out_grad(gg, wo, o):
    blocks, rows, dim = gg.shape
    width = wo.shape[1]
    row = row_spec(rows, width)
    return pl.pallas_call(
        out_grad_kernel, grid=(blocks,), name="out_grad",
        in_specs=[pl.BlockSpec((1, rows, dim), lambda t: (slot_of(t), 0, 0)), whole(wo), row], out_specs=[row, fixed(width, dim)],
        out_shape=[jax.ShapeDtypeStruct(o.shape, BF16), jax.ShapeDtypeStruct((width, dim), F32)],
        compiler_params=params(), cost_estimate=cost(4 * blocks * rows * dim * width, blocks * rows * dim * 2),
    )(gg, wo, o)


def q_grad_kernel(dq_ref, qpre_ref, qn_ref, cos_ref, sin_ref, h_ref, wg_ref, dt_ref):
    @pl.when(grid_step() == 0)
    def _():
        wg_ref[:] = jnp.zeros_like(wg_ref)
        dt_ref[:] = jnp.zeros_like(dt_ref)

    wg_ref[:] += nn(dt_ref[:], h_ref[:])
    cos_t, sin_t = cos_ref[:], sin_ref[:]
    for head in range(2):
        d_pre, _ = head_finish_bwd(qpre_ref[:, lanes(head)], qn_ref[:], cos_t, sin_t, dq_ref[:, lanes(head)].astype(F32))
        dt_ref[lanes(head), :] = d_pre.T.astype(BF16)


def run_q_grad(dq, qpre, chunk, qn, cos_t, sin_t, h, carry=(), key=None):
    seq, dim = h.shape
    rows, height = 512, 256
    count = seq // rows
    row = lambda width, c=0: pl.BlockSpec((rows, width), lambda t: (jnp.minimum(t, count - 1), c))
    specs = [row(256), row(256, chunk), whole(qn), row(HEAD_DIM), row(HEAD_DIM), pl.BlockSpec((rows, dim), lambda t: (jnp.maximum(t - 1, 0), 0))]
    return call(q_grad_kernel, count + 1, specs, [fixed(height, dim)], [jax.ShapeDtypeStruct((height, dim), F32)],
                [pltpu.VMEM((height, rows), BF16)], cost(2 * seq * dim * height, seq * dim * 3), (dq, qpre, qn, cos_t, sin_t, h), carry, key)


def kv_grad_kernel(count, dk_ref, dv_ref, got_ref, kpre_ref, kn_ref, cos_ref, sin_ref, h_ref, o0_ref, o1_ref, wo_ref, kvb_ref, sum_ref, out_ref, dt_ref, acc_ref, land_ref, send, recv):
    step = grid_step()
    me = lax.axis_index('cp')
    is_key = me % 2 == 0
    rows = land_ref.shape[0]
    theirs = pl.multiple_of((1 - (me // 2) % 2) * rows, rows)
    ours = pl.multiple_of((me // 2) % 2 * rows, rows)

    @pl.when(step == 0)
    def _():
        acc_ref[:] = jnp.zeros_like(acc_ref)
        dt_ref[:] = jnp.zeros_like(dt_ref)
        out_ref[:] = jnp.zeros_like(out_ref)

    @pl.when(step <= count)
    def _():
        acc_ref[:] += nn(dt_ref[:], h_ref[:])
        kv = (jnp.where(is_key, dk_ref[:], dv_ref[:]) + got_ref[:]).T.astype(BF16)
        kvb_ref[:] = kv
        dk_pre, _ = head_finish_bwd(kpre_ref[:], kn_ref[:], cos_ref[:], sin_ref[:], kv.astype(F32))
        dt_ref[:] = jnp.where(step < count, jnp.where(is_key, dk_pre, kv.astype(F32)).T, jnp.zeros_like(dk_pre.T)).astype(BF16)

    tokens = o0_ref.shape[3]
    for j in range(2):
        @pl.when(step % 2 == j)
        def _():
            for b in range(2):
                pair = jnp.hstack([o0_ref[0, b, 0][:, lanes(j)], o1_ref[0, b, 0][:, lanes(j)]])
                out_ref[b * tokens:(b + 1) * tokens] += nn(pair, wo_ref[:])

    copy = pltpu.make_async_remote_copy(src_ref=acc_ref.at[pl.ds(theirs, rows)], dst_ref=land_ref, send_sem=send, recv_sem=recv,
                                        device_id=(me ^ 2,), device_id_type=pl.DeviceIdType.MESH)

    @pl.when(step == count + 1)
    def _():
        copy.start()

    @pl.when(step == pl.num_programs(0) - 1)
    def _():
        copy.wait()
        sum_ref[:] = acc_ref[pl.ds(ours, rows), :] + land_ref[:]


def run_kv_grad(dk, dv, got, kpre, kn, cos_t, sin_t, h, o_got, w_out, carry, key):
    seq, dim = h.shape
    rows = 512
    count = seq // rows
    tokens = o_got[0].shape[3]
    last = lambda t: jnp.minimum(t, count - 1)
    col = pl.BlockSpec((HEAD_DIM, rows), lambda t: (0, last(t)))
    row = pl.BlockSpec((rows, HEAD_DIM), lambda t: (last(t), 0))
    src = pl.BlockSpec((1, 2, 1, tokens, 256), lambda s: (s // 4, 0, (s // 2) % 2, 0, 0))
    specs = [col, col, col, row, whole(kn), row, row, pl.BlockSpec((rows, dim), lambda t: (jnp.clip(t - 1, 0, count - 1), 0)),
             src, src, pl.BlockSpec((256, dim), lambda s: (4 * (s // 4) + 2 * (s % 2) + (s // 2) % 2, 0))]
    sds = jax.ShapeDtypeStruct
    half, both = HEAD_DIM // 2, 2 * tokens
    return call(functools.partial(kv_grad_kernel, count), 16, specs, [row, fixed(half, dim), fixed(both, dim)],
                [sds((seq, HEAD_DIM), BF16), sds((half, dim), F32), sds((both, dim), F32)],
                [pltpu.VMEM((HEAD_DIM, rows), BF16), pltpu.VMEM((HEAD_DIM, dim), F32), pltpu.VMEM((half, dim), F32), pltpu.SemaphoreType.DMA, pltpu.SemaphoreType.DMA],
                cost(2 * seq * dim * 768, seq * dim * 2), (dk, dv, got, kpre, kn, cos_t, sin_t, h, *o_got, w_out), carry, key)


def hidden_grad_kernel(final, dq_ref, qa_ref, qb_ref, wa_ref, wb_ref, qn_ref, cos_ref, sin_ref, *refs):
    if final:
        kv_ref, kpre_ref, wk_ref, wv_ref, kn_ref, gain_ref, x_ref, g_ref, so_far_ref, dx_ref, ngq_ref, ngk_ref, ngx_ref, acc_ref, d_ref, w_ref = refs
    else:
        acc_ref, ngq_ref, d_ref = refs
    step = grid_step()
    rows = dq_ref.shape[3]

    @pl.when(step == 0)
    def _():
        acc_ref[:] = so_far_ref[:] if final else jnp.zeros_like(acc_ref)
        ngq_ref[:] = jnp.zeros_like(ngq_ref)
        if final:
            ngk_ref[:] = jnp.zeros_like(ngk_ref)
            ngx_ref[:] = jnp.zeros_like(ngx_ref)

    is_key = step % 2 == 0
    if final:
        w_ref[:] = jnp.where(is_key, wk_ref[:].astype(F32), wv_ref[:].astype(F32)).astype(BF16)
    folded = lambda terms: jnp.sum(terms.reshape(-1, 8, terms.shape[1]), axis=0)
    for b in range(2):
        for first in range(0, rows, HEAD_DIM):
            rs, at = slice(first, first + HEAD_DIM), slice(b * rows + first, b * rows + first + HEAD_DIM)
            cos_t, sin_t = cos_ref[rs], sin_ref[rs]
            for j, q_ref in enumerate((qa_ref, qb_ref)):
                d_pre, terms = head_finish_bwd(q_ref[at], qn_ref[:], cos_t, sin_t, dq_ref[0, b, 0, rs, lanes(j)].astype(F32))
                d_ref[at, lanes(j)] = d_pre.astype(BF16)
                ngq_ref[:] += folded(terms)
            if final:
                kv = kv_ref[0, b, 0, rs].astype(F32)
                dk_pre, terms = head_finish_bwd(kpre_ref[at], kn_ref[:], cos_t, sin_t, kv)
                ngk_ref[:] += jnp.where(is_key, folded(terms), jnp.zeros_like(ngk_ref))
                d_ref[at, lanes(2)] = jnp.where(is_key, dk_pre, kv).astype(BF16)
        at = slice(b * rows, (b + 1) * rows)
        for first in range(0, acc_ref.shape[1], 512):
            cols = slice(first, first + 512)
            part = nt(d_ref[at, :2 * HEAD_DIM], jnp.hstack([wa_ref[cols], wb_ref[cols]]))
            acc_ref[at, cols] += part + nt(d_ref[at, lanes(2)], w_ref[cols]) if final else part
    if not final:
        return

    @pl.when(step == pl.num_programs(0) - 1)
    def _():
        for b in range(2):
            for r in range(0, rows, 64):
                rs = slice(r, r + 64)
                x = x_ref[b, rs].astype(F32)
                scale = row_scale(x)
                unit = x * scale
                d_normed = acc_ref[b * rows + r:b * rows + r + 64, :].astype(BF16).astype(F32)
                ngx_ref[:] += folded(d_normed * unit)
                d_unit = d_normed * gain_ref[:]
                dx_ref[b, rs] = (g_ref[b, rs].astype(F32) + scale * (d_unit - unit * row_mean(d_unit * unit))).astype(BF16)


def run_hidden_grad(dq_got, chunk, qpre_own, w_query, qn, cos_t, sin_t, rest=None, carry=(), key=None):
    rows, dim = dq_got.shape[3], w_query.shape[0]
    both = 2 * rows
    src = lambda width: pl.BlockSpec((1, 2, 1, rows, width), lambda s: (s // 2, 0, s % 2, 0, 0))
    head = lambda height, j: pl.BlockSpec((height, HEAD_DIM), lambda s: (0, 8 * (s // 2) + 4 * j + 2 * (s % 2) + chunk))
    group = lambda height: pl.BlockSpec((height, HEAD_DIM), lambda s: (0, s // 2))
    sds = jax.ShapeDtypeStruct
    norm = sds((8, HEAD_DIM), F32)
    specs = [src(2 * HEAD_DIM), head(both, 0), head(both, 1), head(dim, 0), head(dim, 1), whole(qn), whole(cos_t), whole(sin_t)]
    operands = (dq_got, qpre_own, qpre_own, w_query, w_query, qn, cos_t, sin_t)
    outs = [sds((both, dim), F32), norm]
    scratch = [pltpu.VMEM((both, 3 * HEAD_DIM), BF16)]
    if rest is not None:
        _, _, _, _, kn, gain, hidden_in, grad_out, so_far = rest
        operands += rest
        specs += [src(HEAD_DIM), group(both), group(dim), group(dim), whole(kn), whole(gain), whole(hidden_in), whole(grad_out), whole(so_far)]
        outs = [sds(hidden_in.shape, BF16), norm, norm, sds((8, dim), F32)]
        scratch = [pltpu.VMEM((both, dim), F32)] + scratch + [pltpu.VMEM((dim, HEAD_DIM), BF16)]
    return call(functools.partial(hidden_grad_kernel, rest is not None), 8, specs, [fixed(*out.shape) for out in outs], outs, scratch,
                cost(2 * both * dim * 2560, 30000000), operands, carry, key)


def place_kernel(*refs):
    refs[-1][:] = refs[0][0].T


def run_place(a, chunk, into=None):
    count, height, dim = a.shape[0], HEAD_DIM, a.shape[2]
    more = [] if into is None else [into]
    return pl.pallas_call(
        place_kernel, grid=(count,), name="place",
        in_specs=[pl.BlockSpec((1, height, dim), lambda t: (t, 0, 0))] + [pl.BlockSpec(memory_space=pltpu.HBM)] * len(more),
        out_specs=pl.BlockSpec((dim, height), lambda t: (0, 2 * t + chunk)), input_output_aliases={} if into is None else {1: 0},
        out_shape=jax.ShapeDtypeStruct((dim, 2 * height * count), F32), compiler_params=params(), cost_estimate=cost(1000000, 35000000),
    )(a, *more)


def join_kernel(a_ref, b_ref, y_ref):
    for n in range(a_ref.shape[0]):
        y_ref[2 * n * HEAD_DIM:(2 * n + 1) * HEAD_DIM] = a_ref[n]
        y_ref[(2 * n + 1) * HEAD_DIM:(2 * n + 2) * HEAD_DIM] = b_ref[n]


def run_join(a, b):
    count, height, dim = a.shape
    spec = pl.BlockSpec((2, height, dim), lambda t: (t, 0, 0))
    return pl.pallas_call(
        join_kernel, grid=(count // 2,), name="join", in_specs=[spec, spec], out_specs=pl.BlockSpec((4 * height, dim), lambda t: (t, 0)),
        out_shape=jax.ShapeDtypeStruct((2 * height * count, dim), F32), compiler_params=params(), cost_estimate=cost(1000000, 67000000),
    )(a, b)


def place_kv_kernel(*refs):
    half = HEAD_DIM // 2
    for out in range(2):
        for b in range(2):
            refs[4 + out][:, b * half:(b + 1) * half] = refs[2 * out + b][0].T


def run_place_kv(a):
    dim = a.shape[2]
    source = lambda out, b: pl.BlockSpec((1, HEAD_DIM // 2, dim), lambda g: (4 * g + 2 * b + out, 2, 0))
    spec = pl.BlockSpec((dim, HEAD_DIM), lambda g: (0, g))
    shape = jax.ShapeDtypeStruct((dim, 4 * HEAD_DIM), F32)
    return pl.pallas_call(
        place_kv_kernel, grid=(4,), name="place_kv", in_specs=[source(out, b) for out in range(2) for b in range(2)], out_specs=[spec, spec],
        out_shape=[shape, shape], compiler_params=params(), cost_estimate=cost(1000000, 17000000),
    )(a, a, a, a)


def sum_kernel(x_ref, y_ref, land_ref, send, recv, own):
    me = lax.axis_index('cp')
    meet(me, FLIPS["all"])
    copies = [pltpu.make_async_remote_copy(src_ref=x_ref, dst_ref=land_ref.at[me], send_sem=send.at[n], recv_sem=recv.at[n], device_id=(me ^ flip,),
                                           device_id_type=pl.DeviceIdType.MESH) for n, flip in enumerate(FLIPS["all"])]
    copies.append(pltpu.make_async_copy(x_ref, land_ref.at[me], own))
    for copy in copies:
        copy.start()
    for copy in copies:
        copy.wait()
    total = land_ref[0]
    for n in range(1, 16):
        total = total + land_ref[n]
    y_ref[:] = total


def run_sum(x, key):
    count = pltpu.SemaphoreType.DMA((15,))
    return pl.pallas_call(
        sum_kernel, name="sum", in_specs=[pl.BlockSpec(memory_space=pltpu.HBM)], out_specs=pl.BlockSpec(memory_space=pltpu.VMEM),
        out_shape=jax.ShapeDtypeStruct(x.shape, F32), scratch_shapes=[pltpu.VMEM((16,) + x.shape, F32), count, count, pltpu.SemaphoreType.DMA],
        compiler_params=pltpu.CompilerParams(collective_id=key, has_side_effects=True), cost_estimate=cost(1000000, 1000000),
    )(x)


def solution(mesh):
    n_dev = mesh.shape['cp']
    seq_spec, rep_spec = P(None, 'cp', None), P()
    halves = [[dev for dev in range(n_dev) if (dev >> 1) & 1 == bit] for bit in (0, 1)]

    def local_block(hidden_in, grad_out, w_query, w_key, w_value, w_out, attn_norm, query_norm, key_norm):
        _, seq_dev, dim = hidden_in.shape
        seq = seq_dev * n_dev
        me = lax.axis_index('cp')
        group, which, half = me // 4, (me // 2) % 2, me % 2
        gain = attn_norm.astype(F32).reshape(1, dim)
        qn, kn = query_norm.astype(F32).reshape(1, HEAD_DIM), key_norm.astype(F32).reshape(1, HEAD_DIM)
        keys = iter(range(1, 16))
        blocks = lambda x: x.reshape(-1, seq_dev, x.shape[1])
        by_source = lambda x: x.reshape(4, 2, 2, seq_dev, x.shape[2])
        gather_all = lambda x: lax.all_gather(x, 'cp')
        add_half = lambda parts, got: lax.dynamic_slice_in_dim(parts, which * HEAD_DIM, HEAD_DIM) + got

        qpre_own, kpre_own, cos_t, sin_t, w_all, xg, g_got = run_gather(hidden_in, grad_out, gain, w_query, w_key, w_value, inverse_frequencies(), seq, next(keys))

        head_at = lambda c, j: (8 * group + 4 * j + 2 * half + c) * HEAD_DIM
        wo_mine = [jnp.concatenate([lax.dynamic_slice_in_dim(w_out, head_at(c, j), HEAD_DIM) for j in range(2)]).T for c in range(2)]

        pair = lax.dynamic_update_index_in_dim(grad_out, g_got, 1 - which, 0)
        gg = lax.all_gather(pair, 'cp', axis_index_groups=halves, tiled=True)

        h, qpre, kpre, q, k, kt, v, vt = run_qkv(xg.reshape(seq, dim), gain, w_all, qn, kn, cos_t, sin_t)
        o0, lse0 = run_fwd(q, kt, v, 0)
        do0, wg_o0 = run_out_grad(gg, wo_mine[0], o0)
        dq0, dkt0, dvt0, got = run_bwd(q, do0, o0, lse0, kt, vt, k, 0, [("half", wg_o0)], next(keys), (), (0, 6), False, 'new')
        mine, dkt0 = lax.optimization_barrier((add_half(wg_o0, got), dkt0))
        wg_o0 = gather_all(mine)
        dq0, dkt0, dvt0, o_got0 = run_bwd(q, do0, o0, lse0, kt, vt, k, 0, [("all", blocks(o0))], next(keys), (dkt0, dvt0), (6, 12), False, dq0)
        wg_q0, = run_q_grad(dq0, qpre, 0, qn, cos_t, sin_t, h)

        q, wg_q0 = lax.optimization_barrier((q, wg_q0))
        o1, lse1, got, dq_got0 = run_fwd(q, kt, v, 1, [("half", wg_q0), ("all", blocks(dq0))], next(keys), (0, 9))
        mine, o1 = lax.optimization_barrier((add_half(wg_q0, got), o1))
        wg_q0 = gather_all(mine)
        o1, lse1 = run_fwd(q, kt, v, 1, (), None, (9, 12), (o1, lse1))
        do1, wg_o1 = run_out_grad(gg, wo_mine[1], o1)
        dq1a, dkt, dvt, got, o_got1 = run_bwd(q, do1, o1, lse1, kt, vt, k, 1, [("half", wg_o1), ("all", blocks(o1))], next(keys), (dkt0, dvt0), (0, 9))
        mine, dkt = lax.optimization_barrier((add_half(wg_o1, got), dkt))
        wg_o1 = gather_all(mine)
        dq1b, dkt, dvt, low = run_bwd(q, do1, o1, lse1, kt, vt, k, 1, [("low", blocks(dq1a))], next(keys), (dkt, dvt), (9, 12), True)

        wg_q1, kv_part = run_q_grad(jnp.concatenate([dq1a, dq1b]), qpre, 1, qn, cos_t, sin_t, h, [("other", dkt, dvt)], next(keys))
        kv_b, kv_sum, projected, got = run_kv_grad(dkt, dvt, kv_part, kpre, kn, cos_t, sin_t, h, [by_source(o_got0), by_source(o_got1)], w_out, [("half", wg_q1)], next(keys))
        mine, kv_b = lax.optimization_barrier((jnp.concatenate([add_half(wg_q1, got), kv_sum]), kv_b))
        wg_q1 = gather_all(mine)
        my_cos, my_sin = [lax.dynamic_slice_in_dim(table, me * seq_dev, seq_dev) for table in (cos_t, sin_t)]
        so_far, ng_q0, high, kv_got = run_hidden_grad(by_source(dq_got0), 0, qpre_own, w_query, qn, my_cos, my_sin, None, [("high", blocks(dq1b)), ("all", blocks(kv_b))], next(keys))
        dq_got1 = by_source(jnp.where(me < SPLIT, low, high))
        rest = (by_source(kv_got), kpre_own, w_key, w_value, kn, gain, hidden_in, grad_out, so_far)
        grad_in, ng_q1, ng_k, ng_x = run_hidden_grad(dq_got1, 1, qpre_own, w_query, qn, my_cos, my_sin, rest)
        hidden_out = (hidden_in.astype(F32) + projected.reshape(hidden_in.shape)).astype(BF16)
        wgrad_out = run_join(wg_o0, wg_o1)
        wgrad_q = run_place(wg_q1, 1, run_place(wg_q0, 0))
        wgrad_k, wgrad_v = run_place_kv(wg_q1)
        norms = jnp.sum(jnp.hstack([ng_x, ng_q0 + ng_q1, ng_k]), axis=0, keepdims=True)
        norms, wgrad_k = lax.optimization_barrier((norms, wgrad_k))
        norms = run_sum(norms, next(keys))[0]
        return (hidden_out, grad_in, wgrad_q, wgrad_k, wgrad_v, wgrad_out,
                norms[:dim], norms[dim:dim + HEAD_DIM], norms[dim + HEAD_DIM:])

    return jax.shard_map(local_block, mesh=mesh, in_specs=(seq_spec, seq_spec) + (rep_spec,) * 7, out_specs=(seq_spec, seq_spec) + (rep_spec,) * 7, check_vma=False)
```

time: 1100 us -> 1030 us (0.936)
  Pallas kernels: 781 us -> 968 us
  waiting for transfers between devices: 90 us -> 0.75 us
  local copies, waits for them, and re-layouts: 81.7 us -> 10.9 us
  other arithmetic: 63.4 us -> 26.5 us
  blocking collectives: 33.4 us -> 0 us
  matrix products: 20.3 us -> 0 us
    pallas_call x2 -> x5, Pallas kernels: 95.7 us -> 214 us  [the longest x1 121 us: run_gather(): pl.pallas_call(functools.partial(gather_kernel, steps), grid=(steps,), na...]
    pallas_call x7 -> x12, Pallas kernels: 570 us -> 666 us  [call(): pl.pallas_call(carrying(kernel, len(operands), len(out_shape), len(scratc...]
    ppermute x3 -> x0, waiting for transfers between devices: 73.6 us -> none  [the longest x2 68.2 us: gather_sequence(): got = lax.ppermute(other, 'cp', flip(2))]
    psum x1 -> x0, blocking collectives: 33.4 us -> none  [local_block(): norms = lax.psum(norms, 'cp')]
    unnamed x70 -> x30, local copies, waits for them, and re-layouts: 35.3 us -> 2.8 us
    pallas_call x2, Pallas kernels: 76.4 us -> 49 us  [run_out_grad(): pl.pallas_call(out_grad_kernel, grid=(blocks,), name='out_grad', in_specs...]
    dot_general x2 -> x0, matrix products: 20.3 us -> none  [nn(): lax.dot_general(a, b, (((1,), (0,)), ((), ())), preferred_element_type=F32)]
    all_gather x2 -> x1, waiting for transfers between devices: 15.8 us -> 0.01 us  [local_block(): gg = lax.all_gather(pair, 'cp', axis_index_groups=halves, tiled=True)]
  transfers between devices with their start and end apart: 9 -> 5, of which waited for: 5 -> 0; matrix products, arithmetic and copies ran while one was open for 11% -> 2% of each run, Pallas kernels for 45% -> 56%
where the time goes in v2:
time: 1030 us; the launch traced here: 1020 us
  Pallas kernels  968 us (94%)
  other arithmetic  26.5 us (3%)
  between operations  14.4 us (1%)
  local copies, waits for them, and re-layouts  10.9 us (1%)
    pallas_call x12, Pallas kernels, call(): pl.pallas_call(carrying(kernel, len(operands), len(out_shape), len(scratc...  666 us
    pallas_call x1, Pallas kernels, run_gather(): pl.pallas_call(functools.partial(gather_kernel, steps), grid=(steps,), na...  121 us
    pallas_call x2, Pallas kernels, run_out_grad(): pl.pallas_call(out_grad_kernel, grid=(blocks,), name='out_grad', in_specs...  49 us
    pallas_call x1, Pallas kernels, run_qkv(): pl.pallas_call(qkv_kernel, grid=(seq // rows,), name='qkv', in_specs=[row...  39.9 us
    pallas_call x2, Pallas kernels, run_place(): pl.pallas_call(place_kernel, grid=(count,), name='place', in_specs=[pl.Bl...  38.6 us
    pallas_call x1, Pallas kernels, run_join(): pl.pallas_call(join_kernel, grid=(count // 2,), name='join', in_specs=[sp...  22.8 us
  transfers between devices with their start and end apart: 5, of which 0 were waited for; matrix products, arithmetic and copies ran while one was open for 2% of the time, Pallas kernels for 56%

profile of v2, /device:TPU:0, one launch (start us, length us, event | category | flops | bytes accessed | tf_op | source)
XLA Modules:
  0.0 1021.0 jit_solution(11504573053449787931)
XLA Ops:
  7.3 1.3 reshape.98
  8.6 0.6 maximum_bitcast_fusion.2.freq_ref
  9.1 121.1 %gather.1 = (f32[768,4096]{1,0:T(8,128)}, f32[768,512]{1,0:T(8,128)}, f32[6144,128]{1,0:T(8,128)}, f32[6144,128]{1,0:T(8,128)}, bf16[2048,768]{1,0:T(8,128)(2,1)...) custom-call(bf16[2,384,2048]{2,1,0:T(8,128)(2,1)} %refs_6_.1, f32[1,2048]{1,0:T(1,128)} %bitcast.53, ...), custom_call_target="tpu_custom_call" | custom-call | flops 14495514624 | bytes 60000000 | tf_op jit(solution)/shard_map/gather/pallas_call | solution.py:453
  130.2 1.6 bitcast_dynamic-update-slice_fusion
  131.9 1.7 copy-done
  133.5 0.6 all-gather.14.cloned.1.call-start
  134.2 1.7 constant_dynamic-slice_fusion.3
  135.9 0.3 copy.31
  136.1 0.3 copy.30
  136.4 0.5 bitcast_convert_fusion
  137.0 1.1 maximum_bitcast_fusion.w_ref
  138.1 39.9 %qkv.1 = (bf16[6144,2048]{1,0:T(8,128)(2,1)}, f32[6144,512]{1,0:T(8,128)}, f32[6144,128]{1,0:T(8,128)}, bf16[6144,512]{1,0:T(8,128)(2,1)}, bf16[6144,128]{1,0:T(...) custom-call(bf16[6144,2048]{1,0:T(8,128)(2,1)} %bitcast.57, ...), custom_call_target="tpu_custom_call" | custom-call | flops 19327352832 | bytes 100663296 | tf_op jit(solution)/shard_map/qkv/pallas_call | solution.py:491
  177.9 77.4 %shard_map.160 = (bf16[6144,256]{1,0:T(8,128)(2,1)}, f32[6144,256]{1,0:T(8,128)}) custom-call(bf16[6144,512]{1,0:T(8,128)(2,1)} %get-tuple-element.103.q_ref.refs_0_, bf16[128,6144]{1,0:T(8,128)(2,1)} %get-tuple-element.87.kt_ref.refs_4_.refs_1_, bf16[6144,128]{1,0:T(8,128)(2,1)} %get-tuple-element.88.v_ref.refs_2_), custom_call_target="tpu_custom_call" | custom-call | flops 19327352832 | bytes 25165824 | tf_op jit(solution)/shard_map/pallas_call | solution.py:164
  255.3 24.2 %out_grad.2 = (bf16[6144,256]{1,0:T(8,128)(2,1)}, f32[256,2048]{1,0:T(8,128)}) custom-call(bf16[16,384,2048]{2,1,0:T(8,128)(2,1)} %all-gather.10.cloned.1.call-done.g_ref, bf16[2048,256]{1,0:T(8,128)(2,1)} %maximum_bitcast_fusion.w_ref, bf16[6144,256]{1,0:T(8,128)(2,1)} %get-tuple-element.89.o_ref.refs_2_), custom_call_target="tpu_custom_call" | custom-call | flops 12884901888 | bytes 25165824 | tf_op jit(solution)/shard_map/out_grad/pallas_call | solution.py:515
  279.5 35.2 %shard_map.161 = (bf16[6144,256]{1,0:T(8,128)(2,1)}, f32[128,6144]{1,0:T(8,128)}, f32[128,6144]{1,0:T(8,128)}, f32[128,2048]{1,0:T(8,128)}) custom-call(bf16[6144,512]{1,0:T(8,128)(2,1)} %get-tuple-element.103.q_ref.refs_0_, bf16[6144,256]{1,0:T(8,128)(2,1)} %get-tuple-element.90.refs_1_, bf16[6144,256]{1,0:T(8,128)(2,1)} %get-tuple-element.89.o_ref.refs_2_, ...), custom_call_target="tpu_custom_call" | custom-call | flops 12079595520 | bytes 50331648 | tf_op jit(solution)/shard_map/pallas_call | solution.py:164
  314.7 2.4 dynamic-slice_add_fusion.3
  317.0 83.6 %shard_map.162 = (bf16[6144,256]{1,0:T(8,128)(2,1)}, f32[128,6144]{1,0:T(8,128)}, f32[128,6144]{1,0:T(8,128)}, bf16[16,384,256]{2,1,0:T(8,128)(2,1)}) custom-call(bf16[6144,512]{1,0:T(8,128)(2,1)} %get-tuple-element.103.q_ref.refs_0_, bf16[6144,256]{1,0:T(8,128)(2,1)} %get-tuple-element.90.refs_1_, ...), custom_call_target="tpu_custom_call", output_to_operand_aliasing={{0}: (9, {})} | custom-call | flops 36238786560 | bytes 50331648 | tf_op jit(solution)/shard_map/pallas_call | solution.py:164
  400.6 21.8 %shard_map.163.refs_3_ = f32[256,2048]{1,0:T(8,128)} custom-call(bf16[6144,256]{1,0:T(8,128)(2,1)} %get-tuple-element.100.dq_ref, f32[6144,512]{1,0:T(8,128)} %get-tuple-element.101.qpre_ref.refs_1_, f32[1,128]{1,0:T(1,128)} %get-tuple-element.162.qn_ref.refs_2_.refs_5_, f32[6144,128]{1,0:T(8,128)} %get-tuple-element.83.cos_ref.refs_3_.refs_5_, ...), custom_call_target="tpu_custom_call" | custom-call | flops 6442450944 | bytes 37748736 | tf_op jit(solution)/shard_map/pallas_call | solution.py:164
  422.4 64.3 %shard_map.164 = (bf16[6144,256]{1,0:T(8,128)(2,1)}, f32[6144,256]{1,0:T(8,128)}, f32[128,2048]{1,0:T(8,128)}, bf16[16,384,256]{2,1,0:T(8,128)(2,1)}) custom-call(bf16[6144,512]{1,0:T(8,128)(2,1)} %get-tuple-element.103.q_ref.refs_0_, bf16[128,6144]{1,0:T(8,128)(2,1)} %get-tuple-element.87.kt_ref.refs_4_.refs_1_, ...), custom_call_target="tpu_custom_call" | custom-call | flops 10871635968 | bytes 25165824 | tf_op jit(solution)/shard_map/pallas_call | solution.py:164
  486.6 2.3 dynamic-slice_add_fusion.2
  489.0 0.7 all-gather.16.cloned.1.call-update
  490.0 0.3 copy.32
  490.3 1.1 maximum_bitcast_fusion.1.w_ref
  491.4 32.9 %shard_map.165 = (bf16[6144,256]{1,0:T(8,128)(2,1)}, f32[6144,256]{1,0:T(8,128)}) custom-call(bf16[6144,512]{1,0:T(8,128)(2,1)} %get-tuple-element.103.q_ref.refs_0_, bf16[128,6144]{1,0:T(8,128)(2,1)} %get-tuple-element.87.kt_ref.refs_4_.refs_1_, bf16[6144,128]{1,0:T(8,128)(2,1)} %get-tuple-element.88.v_ref.refs_2_, ...), custom_call_target="tpu_custom_call", output_to_operand_aliasing={{0}: (3, {}), {1}: (4, {})} | custom-call | flops 8455716864 | bytes 25165824 | tf_op jit(solution)/shard_map/pallas_call | solution.py:164
  524.3 24.9 %out_grad.3 = (bf16[6144,256]{1,0:T(8,128)(2,1)}, f32[256,2048]{1,0:T(8,128)}) custom-call(bf16[16,384,2048]{2,1,0:T(8,128)(2,1)} %all-gather.10.cloned.1.call-done.g_ref, bf16[2048,256]{1,0:T(8,128)(2,1)} %maximum_bitcast_fusion.1.w_ref, bf16[6144,256]{1,0:T(8,128)(2,1)} %get-tuple-element.109.o_ref.refs_2_), custom_call_target="tpu_custom_call" | custom-call | flops 12884901888 | bytes 25165824 | tf_op jit(solution)/shard_map/out_grad/pallas_call | solution.py:515
  549.2 99.5 %shard_map.166 = (bf16[4608,256]{1,0:T(8,128)(2,1)}, f32[128,6144]{1,0:T(8,128)}, f32[128,6144]{1,0:T(8,128)}, f32[128,2048]{1,0:T(8,128)}, bf16[16,384,256]{2,1,0:T(8,128)(2,1)}) custom-call(bf16[6144,512]{1,0:T(8,128)(2,1)} %get-tuple-element.103.q_ref.refs_0_, bf16[6144,256]{1,0:T(8,128)(2,1)} %get-tuple-element.110.refs_1_, ...), custom_call_target="tpu_custom_call" | custom-call | flops 27179089920 | bytes 50331648 | tf_op jit(solution)/shard_map/pallas_call | solution.py:164
  648.7 2.3 dynamic-slice_add_fusion.1
  651.2 58.5 %shard_map.167 = (bf16[1536,256]{1,0:T(8,128)(2,1)}, f32[128,6144]{1,0:T(8,128)}, f32[128,6144]{1,0:T(8,128)}, bf16[16,384,256]{2,1,0:T(8,128)(2,1)}) custom-call(bf16[6144,512]{1,0:T(8,128)(2,1)} %get-tuple-element.103.q_ref.refs_0_, bf16[6144,256]{1,0:T(8,128)(2,1)} %get-tuple-element.110.refs_1_, bf16[6144,256]{1,0:T(8,128)(2,1)} %get-tuple-element.109.o_ref.refs_2_, ...), custom_call_target="tpu_custom_call" | custom-call | flops 21139292160 | bytes 50331648 | tf_op jit(solution)/shard_map/pallas_call | solution.py:164
  709.7 3.0 pad_maximum_fusion.refs_0_
  712.7 22.6 %shard_map.168 = (f32[256,2048]{1,0:T(8,128)}, f32[128,6144]{1,0:T(8,128)}) custom-call(bf16[6144,256]{1,0:T(8,128)(2,1)} %pad_maximum_fusion.refs_0_, f32[6144,512]{1,0:T(8,128)} %get-tuple-element.101.qpre_ref.refs_1_, f32[1,128]{1,0:T(1,128)} %get-tuple-element.162.qn_ref.refs_2_.refs_5_, f32[6144,128]{1,0:T(8,128)} %get-tuple-element.83.cos_ref.refs_3_.refs_5_, ...), custom_call_target="tpu_custom_call" | custom-call | flops 6442450944 | bytes 37748736 | tf_op jit(solution)/shard_map/pallas_call | solution.py:164
  735.3 67.4 %shard_map.169 = (bf16[6144,128]{1,0:T(8,128)(2,1)}, f32[64,2048]{1,0:T(8,128)}, f32[768,2048]{1,0:T(8,128)}, f32[128,2048]{1,0:T(8,128)}) custom-call(f32[128,6144]{1,0:T(8,128)} %get-tuple-element.120.refs_6_.refs_0_, f32[128,6144]{1,0:T(8,128)} %get-tuple-element.121.refs_7_.refs_1_, f32[128,6144]{1,0:T(8,128)} %get-tuple-element.123.refs_2_, ...), custom_call_target="tpu_custom_call" | custom-call | flops 19327352832 | bytes 25165824 | tf_op jit(solution)/shard_map/pallas_call | solution.py:164
  802.7 1.4 dynamic-slice_add_fusion
  804.2 1.2 pad_maximum_fusion.1
  805.5 1.8 constant_dynamic-slice_fusion
  807.2 60.7 %shard_map.170 = (f32[768,2048]{1,0:T(8,128)}, f32[8,128]{1,0:T(8,128)}, bf16[16,384,256]{2,1,0:T(8,128)(2,1)}, bf16[16,384,128]{2,1,0:T(8,128)(2,1)}) custom-call(bf16[4,2,2,384,256]{4,3,2,1,0:T(8,128)(2,1)} %bitcast.48, f32[768,4096]{1,0:T(8,128)} %get-tuple-element.131.refs_1_.refs_2_.qa_ref.qb_ref, ...), custom_call_target="tpu_custom_call" | custom-call | flops 8053063680 | bytes 30000000 | tf_op jit(solution)/shard_map/pallas_call | solution.py:164
  867.9 2.0 broadcast_select_fusion
  869.9 42.6 %shard_map.171 = (bf16[2,384,2048]{2,1,0:T(8,128)(2,1)}, f32[8,128]{1,0:T(8,128)}, f32[8,128]{1,0:T(8,128)}, f32[8,2048]{1,0:T(8,128)}) custom-call(bf16[4,2,2,384,256]{4,3,2,1,0:T(8,128)(2,1)} %bitcast.45, f32[768,4096]{1,0:T(8,128)} %get-tuple-element.131.refs_1_.refs_2_.qa_ref.qb_ref, f32[768,4096]{1,0:T(8,128)} %get-tuple-element.131.refs_1_.refs_2_.qa_ref.qb_ref, ...), custom_call_target="tpu_custom_call" | custom-call | flops 8053063680 | bytes 30000000 | tf_op jit(solution)/shard_map/pallas_call | solution.py:164
  912.6 0.7 add.91
  913.2 0.9 maximum_reduce_fusion
  914.1 0.6 broadcast_in_dim.8.x_ref
  914.7 5.7 add_convert_fusion
  920.4 19.4 %place.2.refs_1_ = f32[2048,4096]{1,0:T(8,128)} custom-call(f32[16,128,2048]{2,1,0:T(8,128)} %bitcast.42), custom_call_target="tpu_custom_call" | custom-call | flops 1000000 | bytes 35000000 | tf_op jit(solution)/shard_map/place/pallas_call | solution.py:692
  939.8 22.8 %join.1 = f32[4096,2048]{1,0:T(8,128)} custom-call(f32[16,128,2048]{2,1,0:T(8,128)} %bitcast.43, f32[16,128,2048]{2,1,0:T(8,128)} %bitcast.44), custom_call_target="tpu_custom_call" | custom-call | flops 1000000 | bytes 67000000 | tf_op jit(solution)/shard_map/join/pallas_call | solution.py:709
  962.6 9.8 place_kv.1
  972.4 20.2 %sum.1 = f32[1,2304]{1,0:T(1,128)} custom-call(f32[1,2304]{1,0:T(1,128)} %broadcast_in_dim.8.x_ref), custom_call_target="tpu_custom_call" | custom-call | flops 1000000 | bytes 1000000 | tf_op jit(solution)/shard_map/sum/pallas_call | solution.py:751
  992.5 1.3 slice.18
  993.8 1.2 slice_bitcast_fusion
  995.0 19.2 %place.3 = f32[2048,4096]{1,0:T(8,128)} custom-call(f32[16,192,2048]{2,1,0:T(8,128)} %bitcast.41, f32[2048,4096]{1,0:T(8,128)} %place.2.refs_1_), custom_call_target="tpu_custom_call", output_to_operand_aliasing={{}: (1, {})} | custom-call | flops 1000000 | bytes 35000000 | tf_op jit(solution)/shard_map/place/pallas_call | solution.py:692
  (40 shorter events, 0.6 us)
Async XLA Ops:
  7.2 248.2 %all-gather.10.cloned.1.call-start = ((), (), s32[]{:S(2)}) async-start(), calls=%async_computation | async-start | bytes 28311552 | tf_op jit(solution)/shard_map/all_gather | solution.py:782
  9.1 121.1 %copy-start.1 = (bf16[2,384,2048]{2,1,0:T(8,128)(2,1)S(1)}, bf16[2,384,2048]{2,1,0:T(8,128)(2,1)}, u32[]{:S(2)}) copy-start(bf16[2,384,2048]{2,1,0:T(8,128)(2,1)} %refs_7_.1) | copy-start | bytes 9437188
  131.8 1.7 copy-start
  133.5 786.9 %all-gather.14.cloned.1.call-start = ((), (), s32[]{:S(2)}) async-start(), calls=%async_computation.2 | async-start | bytes 17825792 | tf_op jit(solution)/shard_map/all_gather | solution.py:773
  134.2 2.3 copy-start.11
  134.2 2.3 copy-start.12
  279.5 35.2 %copy-start.8 = (f32[256,2048]{1,0:T(8,128)S(1)}, f32[256,2048]{1,0:T(8,128)}, u32[]{:S(2)}) copy-start(f32[256,2048]{1,0:T(8,128)} %get-tuple-element.94.refs_7_) | copy-start | bytes 6291460
  422.4 64.3 %copy-start.3 = (f32[256,2048]{1,0:T(8,128)S(1)}, f32[256,2048]{1,0:T(8,128)}, u32[]{:S(2)}) copy-start(f32[256,2048]{1,0:T(8,128)} %shard_map.163.refs_3_) | copy-start | bytes 6291460
  489.0 450.8 %all-gather.16.cloned.1.call-start = ((), (), s32[]{:S(2)}) async-start(), calls=%async_computation.3 | async-start | bytes 17825792 | tf_op jit(solution)/shard_map/all_gather | solution.py:773
  489.7 450.1 %all-gather.18.cloned.1.call-start = ((), (), s32[]{:S(2)}) async-start(), calls=%async_computation.4 | async-start | bytes 17825792 | tf_op jit(solution)/shard_map/all_gather | solution.py:773
  549.2 99.5 %copy-start.7 = (f32[256,2048]{1,0:T(8,128)S(1)}, f32[256,2048]{1,0:T(8,128)}, u32[]{:S(2)}) copy-start(f32[256,2048]{1,0:T(8,128)} %get-tuple-element.112.refs_9_) | copy-start | bytes 6291460
  651.1 311.5 %all-gather.12.cloned.1.call-start = ((), (), s32[]{:S(2)}) async-start(), calls=%async_computation.1 | async-start | bytes 26738688 | tf_op jit(solution)/shard_map/all_gather | solution.py:773
  651.2 58.5 %copy-start.5 = (bf16[4608,256]{1,0:T(8,128)(2,1)S(1)}, bf16[4608,256]{1,0:T(8,128)(2,1)}, u32[]{:S(2)}) copy-start(bf16[4608,256]{1,0:T(8,128)(2,1)} %get-tuple-element.119) | copy-start | bytes 7077892
  735.3 67.5 %copy-start.6 = (f32[256,2048]{1,0:T(8,128)S(1)}, f32[256,2048]{1,0:T(8,128)}, u32[]{:S(2)}) copy-start(f32[256,2048]{1,0:T(8,128)} %get-tuple-element.127.refs_11_) | copy-start | bytes 6291460
  802.7 1.5 copy-start.9
  807.2 60.7 %copy-start.4 = (bf16[16,384,256]{2,1,0:T(8,128)(2,1)S(1)}, bf16[16,384,256]{2,1,0:T(8,128)(2,1)}, u32[]{:S(2)}) copy-start(bf16[16,384,256]{2,1,0:T(8,128)(2,1)} %get-tuple-element.129) | copy-start | bytes 9437188
  869.9 42.6 %copy-start.10 = (f32[8,128]{1,0:T(8,128)S(1)}, f32[8,128]{1,0:T(8,128)}, u32[]{:S(2)}) copy-start(f32[8,128]{1,0:T(8,128)} %get-tuple-element.144) | copy-start | bytes 12292
  869.9 44.8 %copy-start.2 = (bf16[2,384,2048]{2,1,0:T(8,128)(2,1)S(1)}, bf16[2,384,2048]{2,1,0:T(8,128)(2,1)}, u32[]{:S(2)}) copy-start(bf16[2,384,2048]{2,1,0:T(8,128)(2,1)} %refs_6_.1) | copy-start | bytes 9437188
Sparse Core Ops, SparseCore 0:
  133.7 120.5 all-gather.9
  489.1 78.6 all-gather.13
  570.1 137.7 all-gather.15
  710.5 103.0 all-gather.17
  816.3 140.0 all-gather.11
